TPU v7x, 128 devices: a whole 4x4x4 slice. The times are simulated.
128 devices in a mesh: gx: 16 (over y, x), gy: 2 (over core), gz: 4 (over z).
Axes of the slice: x: 4, y: 4, z: 4, core: 2. Of those that a mesh axis runs over, the one named last changes fastest.
Arguments:
- potential: float32 [960, 120, 512], P('gx', 'gy', 'gz'), may hold values from -6 to 6
- frag_root: int32 [3, 512], P(None, ('gx', 'gy', 'gz')), may hold values from 0 to 959, as said below
Outputs:
- frag_fields: float32 [512, 110592], P(('gx', 'gy', 'gz'))
Inputs may be any that keep to these rules, and one draw needn't show every extreme that they name: `frag_root`: fragment f is held by the device of linear index f // 4 (gx slowest). Along each dimension the box's first cell is the start of a block plus an offset in [-34, B - 34), B being that dimension's cells of one device. Along y and z that block is the holding device's own; along x it is the block of some device with the same gy and gz index, the anchor. Every anchor of a device supplies exactly 1 of its fragments.
All inputs are finite; a program needn't handle non-finite values.
Results may differ from a plain program's by a relative error of at most 0.00007.
Values sent between devices are 32-bit elements; how exact they have to be, the bound alone decides.
A program may use at most 320 MiB of HBM per device.

v0:
```python
import math

import jax
import jax.numpy as jnp
from jax import lax
from jax.sharding import PartitionSpec as P

G = 48
CAP = 1
BOX = 68
HALO = 34


def padded(array, sides, width):
    for axis, dim in sides:
        devices, length = (lax.axis_size(axis), array.shape[dim])
        up = [(i, (i + 1) % devices) for i in range(devices)]
        down = [(j, i) for i, j in up]
        last = lax.slice_in_dim(array, length - width, length, axis=dim)
        initial = lax.slice_in_dim(array, 0, width, axis=dim)
        before = lax.ppermute(last, axis, up)
        after = lax.ppermute(initial, axis, down)
        array = jnp.concatenate([before, array, after], axis=dim)
    return array


def from_everyone(array, axis):
    devices = lax.axis_size(axis)
    return lax.all_to_all(
        jnp.broadcast_to(array[None], (devices, *array.shape)), axis, 0, 0, tiled=True
    )


def laid_out(blocks, dim):
    shape = list(blocks.shape[1:])
    shape[dim] *= blocks.shape[0]
    return jnp.moveaxis(blocks, 0, dim).reshape(shape)


def gathered_copies(array, axis, dim):
    blocks = from_everyone(array, axis)
    return laid_out(blocks, dim)


def interp_table(points, cells):
    row_index = jnp.arange(points, dtype=jnp.int32)[:, None]
    col_index = jnp.arange(cells, dtype=jnp.int32)[None, :]
    offset = row_index * cells - col_index * points
    period = points * cells
    summed = jnp.ones((points, cells), jnp.float32)
    for harmonic in range(1, points // 2):
        phase_angle = jnp.mod(harmonic * offset, period).astype(jnp.float32)
        summed = summed + 2.0 * jnp.cos(2.0 * math.pi / period * phase_angle)
    return summed / cells


def refine(window, matrix):
    highest = lax.Precision.HIGHEST
    step_x = jnp.einsum("ax,xyz->ayz", matrix, window, precision=highest)
    step_y = jnp.einsum("by,ayz->abz", matrix, step_x, precision=highest)
    step_z = jnp.einsum("cz,abz->abc", matrix, step_y, precision=highest)
    return step_z.reshape(-1)


def anchor_ranks(root, total_x, along_x, slot_count):
    anchor = jnp.mod(root[0] + HALO, total_x) // along_x
    grouped = anchor.reshape(-1, slot_count)
    matches = grouped[:, :, None] == grouped[:, None, :]
    earlier = jnp.arange(slot_count)[None, :] < jnp.arange(slot_count)[:, None]
    ordering = jnp.sum(jnp.logical_and(matches, earlier[None, :, :]).astype(jnp.int32), axis=2)
    return (grouped, ordering)


def body(potential, frag_root):
    along_x, along_y, along_z = potential.shape
    groups = lax.axis_size("gx")
    total_x = along_x * groups
    total_y = along_y * lax.axis_size("gy")
    total_z = along_z * lax.axis_size("gz")
    place_x = lax.axis_index("gx")
    place_y = lax.axis_index("gy")
    place_z = lax.axis_index("gz")
    slot_count = frag_root.shape[1]
    matrix = interp_table(G, BOX)
    extended = padded(potential, (("gx", 0), ("gy", 1), ("gz", 2)), HALO)
    line_root = gathered_copies(frag_root, "gx", 1)
    line_anchor, line_rank = anchor_ranks(line_root, total_x, along_x, slot_count)
    start_x = jnp.mod(line_root[0] + HALO - place_x * along_x, total_x).reshape(groups, slot_count)
    start_y = jnp.mod(line_root[1] + HALO - place_y * along_y, total_y).reshape(groups, slot_count)
    start_z = jnp.mod(line_root[2] + HALO - place_z * along_z, total_z).reshape(groups, slot_count)
    chosen = jnp.logical_and(
        line_anchor[:, None, :] == place_x,
        line_rank[:, None, :] == jnp.arange(CAP, dtype=jnp.int32)[None, :, None],
    )

    def select_slots(values):
        return jnp.sum(jnp.where(chosen, values[:, None, :], 0), axis=2).reshape(-1)

    def cut_window(corner_x, corner_y, corner_z):
        return lax.dynamic_slice(extended, (corner_x, corner_y, corner_z), (BOX, BOX, BOX))

    windows = jax.vmap(cut_window)(
        select_slots(start_x), select_slots(start_y), select_slots(start_z)
    )
    own_anchor, own_rank = anchor_ranks(frag_root, total_x, along_x, slot_count)
    own_index = (own_anchor * CAP + own_rank).reshape(-1)
    fields = jax.vmap(refine, in_axes=(0, None))(windows, matrix)
    received = lax.all_to_all(
        fields.reshape(groups, CAP, G * G * G), "gx", split_axis=0, concat_axis=0, tiled=True
    )
    return jnp.take(received.reshape(groups * CAP, G * G * G), own_index, axis=0)


def solution(mesh):
    return jax.shard_map(
        body,
        mesh=mesh,
        in_specs=(P("gx", "gy", "gz"), P(None, ("gx", "gy", "gz"))),
        out_specs=P(("gx", "gy", "gz"), None),
        check_vma=False,
    )
```

profile of v0, /device:TPU:1, one launch (start us, length us, event | category | flops | bytes accessed | tf_op | source)
XLA Modules:
  0.0 547.6 jit_solution(14495292831839624307)
XLA Ops:
  1.7 2.1 collective-permute-start
  3.8 3.8 collective-permute-start.1
  7.6 2.6 copy.56
  10.3 21.5 %collective-permute-done = f32[34,60,128]{2,1,0:T(8,128)S(1)} collective-permute-done((f32[34,60,128]{2,1,0:T(8,128)S(1)}, f32[34,60,128]{2,1,0:T(8,128)S(1)}, u32[]{:S(2)}, u32[]{:S(2)}) %collective-permute-start) | collective-permute-done | bytes 1044512 | tf_op jit(solution)/shard_map/ppermute | solution.py:21
  35.6 3.9 collective-permute-done.2
  39.5 3.2 collective-permute-done.3
  42.7 3.0 pad_maximum_fusion.1
  45.7 7.3 %fusion.241 = (f32[128,128,34]{2,0,1:T(8,128)}, f32[128,128,34]{2,0,1:T(8,128)}) fusion(f32[128,128,128]{2,0,1:T(8,128)S(1)} %pad_maximum_fusion.1), kind=kLoop, calls=%fused_computation.336 | loop fusion | bytes 8912896 | tf_op jit(solution)/shard_map/slice | solution.py:19
  53.0 8.1 %copy.58 = f32[128,128,34]{1,0,2:T(8,128)} copy(f32[128,128,34]{2,0,1:T(8,128)} %get-tuple-element.45) | data formatting | bytes 4456448 | tf_op jit(solution)/shard_map/slice | solution.py:19
  62.8 8.1 %copy.59 = f32[128,128,34]{1,0,2:T(8,128)} copy(f32[128,128,34]{2,0,1:T(8,128)} %get-tuple-element.46) | data formatting | bytes 4456448 | tf_op jit(solution)/shard_map/slice | solution.py:20
  70.9 2.1 collective-permute-start.5
  73.6 5.8 %all-to-all-start = ((s32[16,3,4]{2,1,0:T(4,128)}), s32[16,3,4]{2,1,0:T(4,128)S(1)}, u32[]{:S(2)}, u32[]{:S(2)}) async-start(s32[16,3,4]{2,1,0:T(4,128)} %broadcast_in_dim.17), calls=%async_computation | async-start | bytes 65536 | tf_op jit(solution)/shard_map/all_to_all | solution.py:29
  79.5 6.4 %all-to-all-done = s32[16,3,4]{2,1,0:T(4,128)S(1)} async-done(((s32[16,3,4]{2,1,0:T(4,128)}), s32[16,3,4]{2,1,0:T(4,128)S(1)}, u32[]{:S(2)}, u32[]{:S(2)}) %all-to-all-start) | async-done | bytes 800 | tf_op jit(solution)/shard_map/all_to_all | solution.py:29
  86.2 27.5 %collective-permute-done.4 = f32[128,128,34]{1,0,2:T(8,128)} collective-permute-done((f32[128,128,34]{1,0,2:T(8,128)}, f32[128,128,34]{1,0,2:T(8,128)}, u32[]{:S(2)}, u32[]{:S(2)}) %collective-permute-start.4) | collective-permute-done | bytes 2228256 | tf_op jit(solution)/shard_map/ppermute | solution.py:21
  113.6 8.6 %copy.60 = f32[128,128,34]{2,0,1:T(8,128)} copy(f32[128,128,34]{1,0,2:T(8,128)} %collective-permute-done.4) | data formatting | bytes 4456448 | tf_op jit(solution)/shard_map/ppermute | solution.py:21
  122.3 8.6 %copy.61 = f32[128,128,34]{2,0,1:T(8,128)} copy(f32[128,128,34]{1,0,2:T(8,128)} %collective-permute-done.5) | data formatting | bytes 4456448 | tf_op jit(solution)/shard_map/ppermute | solution.py:22
  130.9 21.7 %pad_maximum_fusion = f32[128,128,196]{2,0,1:T(8,128)} fusion(f32[128,128,34]{2,0,1:T(8,128)} %copy.61, f32[128,34,128]{2,0,1:T(8,128)} %copy-done.2, f32[34,60,128]{2,0,1:T(8,128)} %copy-done, f32[60,60,128]{2,0,1:T(8,128)S(1)} %copy.56, f32[34,60,128]{2,0,1:T(8,128)S(1)} %copy.55, f32[128,34,128]{2,0,1:T(8,128)} %copy-done.1, f32[128,128,34]{2,0,1:T(8,128)} %copy.60), kind=kLoop, calls=%fused_computation.8 | loop fusion | flops 19267584 | bytes 25690112 | tf_op jit(solution)/shard_map/concatenate | solution.py:23
  152.5 131.8 %while.1 = (s32[]{:T(128)}, f32[128,128,196]{2,0,1:T(8,128)}, s32[16,3]{0,1:T(4,128)S(1)}, f32[16,68,68,68]{3,1,2,0:T(8,128)}, s32[]{:T(128)}) while((s32[]{:T(128)}, f32[128,128,196]{2,0,1:T(8,128)}, s32[16,3]{0,1:T(4,128)S(1)}, f32[16,68,68,68]{3,1,2,0:T(8,128)}, s32[]{:T(128)}) %tuple.31), condition=%wide.while_cond, body=%wide.while_body.sunk | while | flops 2 | bytes 8796021 | solution.py:100
  153.2 5.2 dynamic-slice.7
  161.4 5.2 dynamic-slice.7
  167.1 1.9 copy_dynamic-update-slice_fusion.2
  169.7 5.2 dynamic-slice.7
  175.4 1.9 copy_dynamic-update-slice_fusion.2
  177.9 5.2 dynamic-slice.7
  183.6 1.9 copy_dynamic-update-slice_fusion.2
  186.2 5.2 dynamic-slice.7
  194.4 5.2 dynamic-slice.7
  202.6 5.2 dynamic-slice.7
  210.8 5.2 dynamic-slice.7
  219.1 5.2 dynamic-slice.7
  224.7 1.9 copy_dynamic-update-slice_fusion.2
  227.3 5.2 dynamic-slice.7
  235.5 5.2 dynamic-slice.7
  241.2 2.0 copy_dynamic-update-slice_fusion.2
  243.9 5.2 dynamic-slice.7
  249.5 2.0 copy_dynamic-update-slice_fusion.2
  252.2 5.2 dynamic-slice.7
  260.4 5.2 dynamic-slice.7
  268.6 5.2 dynamic-slice.7
  276.8 5.2 dynamic-slice.7
  284.4 42.6 %fusion.191 = f32[48,16,68,68]{3,0,2,1:T(8,128)} fusion(f32[16,68,68,68]{3,1,2,0:T(8,128)} %get-tuple-element.12, s32[68]{0:T(128)S(1)} %iota_multiply_fusion, s32[48]{0:T(128)S(1)} %iota_multiply_fusion.1), kind=kOutput, calls=%fused_computation.245 | convolution fusion | flops 2898634240 | bytes 34329040 | tf_op jit(solution)/shard_map/vmap(ax,xyz->ayz)/dot_general | solution.py:59
  327.0 45.9 %fusion = f32[48,16,68,48]{2,3,0,1:T(8,128)S(1)} fusion(f32[48,16,68,68]{3,0,2,1:T(8,128)} %fusion.191, s32[68]{0:T(128)S(1)} %iota_multiply_fusion, s32[48]{0:T(128)S(1)} %iota_multiply_fusion.1), kind=kOutput, calls=%fused_computation.4 | convolution fusion | flops 2046338688 | bytes 24232400 | tf_op jit(solution)/shard_map/vmap(by,ayz->abz)/dot_general | solution.py:60
  372.9 25.6 %fusion.2 = f32[16,48,48,48]{3,2,1,0:T(8,128)} fusion(f32[48,16,68,48]{2,3,0,1:T(8,128)S(1)} %fusion, s32[68]{0:T(128)S(1)} %iota_multiply_fusion, s32[48]{0:T(128)S(1)} %iota_multiply_fusion.1), kind=kOutput, calls=%fused_computation.6 | convolution fusion | flops 1444718208 | bytes 17105360 | tf_op jit(solution)/shard_map/vmap(cz,abz->abc)/dot_general | solution.py:61
  398.5 22.5 %reshape.517 = f32[16,1,110592]{2,1,0:T(1,128)} reshape(f32[16,48,48,48]{3,2,1,0:T(8,128)} %fusion.2) | data formatting | bytes 14155776 | tf_op jit(solution)/shard_map/reshape;vmap()/reshape | solution.py:109
  421.1 5.7 %all-to-all-start.1 = ((f32[16,1,110592]{2,1,0:T(1,128)}), f32[16,1,110592]{2,1,0:T(1,128)}, u32[]{:S(2)}, u32[]{:S(2)}) async-start(f32[16,1,110592]{2,1,0:T(1,128)} %reshape.517), calls=%async_computation.1 | async-start | bytes 14155776 | tf_op jit(solution)/shard_map/all_to_all | solution.py:108
  427.0 103.2 %all-to-all-done.1 = f32[16,1,110592]{2,1,0:T(1,128)} async-done(((f32[16,1,110592]{2,1,0:T(1,128)}), f32[16,1,110592]{2,1,0:T(1,128)}, u32[]{:S(2)}, u32[]{:S(2)}) %all-to-all-start.1) | async-done | bytes 7077920 | tf_op jit(solution)/shard_map/all_to_all | solution.py:108
  530.2 10.0 %copy.78 = f32[16,1,110592]{2,0,1:T(8,128)} copy(f32[16,1,110592]{2,1,0:T(1,128)} %all-to-all-done.1) | data formatting | bytes 14155776
  540.3 5.2 gather_fusion
  (94 shorter events, 46.8 us)
Async XLA Ops:
  1.7 30.1 %collective-permute-start = (f32[34,60,128]{2,1,0:T(8,128)S(1)}, f32[34,60,128]{2,1,0:T(8,128)S(1)}, u32[]{:S(2)}, u32[]{:S(2)}) collective-permute-start(f32[34,60,128]{2,1,0:T(8,128)S(1)} %get-tuple-element.49), channel_id=1, source_target_pairs={{0,8},{8,16},{16,24},{24,32},{32,40},{40,48},{48,56},{56,64},{64,7... | collective-permute-start | bytes 3133448 | tf_op jit(solution)/shard_map/ppermute | solution.py:21
  3.8 28.6 %collective-permute-start.1 = (f32[34,60,128]{2,1,0:T(8,128)S(1)}, f32[34,60,128]{2,1,0:T(8,128)S(1)}, u32[]{:S(2)}, u32[]{:S(2)}) collective-permute-start(f32[34,60,128]{2,1,0:T(8,128)S(1)} %get-tuple-element.50), channel_id=1, source_target_pairs={{8,0},{16,8},{24,16},{32,24},{40,32},{48,40},{56,48},{64,56},{72,6... | collective-permute-start | bytes 3133448 | tf_op jit(solution)/shard_map/ppermute | solution.py:22
  33.1 9.6 %copy-start = (f32[34,60,128]{2,0,1:T(8,128)}, f32[34,60,128]{2,0,1:T(8,128)S(1)}, u32[]{:S(2)}) copy-start(f32[34,60,128]{2,0,1:T(8,128)S(1)} %copy.57) | copy-start | bytes 3133444
  34.2 5.3 collective-permute-start.2
  35.5 7.2 %collective-permute-start.3 = (f32[128,34,128]{2,0,1:T(8,128)S(1)}, f32[128,34,128]{2,0,1:T(8,128)S(1)}, u32[]{:S(2)}, u32[]{:S(2)}) collective-permute-start(f32[128,34,128]{2,0,1:T(8,128)S(1)} %get-tuple-element.48), channel_id=1, source_target_pairs={{4,0},{0,4},{5,1},{1,5},{6,2},{2,6},{7,3},{3,7},{12,8},{8,12},{13,... | collective-permute-start | bytes 6684680 | tf_op jit(solution)/shard_map/ppermute | solution.py:22
  39.5 6.2 %copy-start.1 = (f32[128,34,128]{2,0,1:T(8,128)}, f32[128,34,128]{2,0,1:T(8,128)S(1)}, u32[]{:S(2)}) copy-start(f32[128,34,128]{2,0,1:T(8,128)S(1)} %collective-permute-done.2) | copy-start | bytes 6684676
  42.7 3.0 copy-start.2
  61.1 11.9 %copy-start.3 = (s32[3,4]{1,0:T(4,128)S(1)}, s32[3,4]{1,0:T(4,128)}, u32[]{:S(2)}) copy-start(s32[3,4]{1,0:T(4,128)} %param.3) | copy-start | bytes 148
  61.1 52.5 %collective-permute-start.4 = (f32[128,128,34]{1,0,2:T(8,128)}, f32[128,128,34]{1,0,2:T(8,128)}, u32[]{:S(2)}, u32[]{:S(2)}) collective-permute-start(f32[128,128,34]{1,0,2:T(8,128)} %copy.58), channel_id=1, source_target_pairs={{0,1},{1,2},{2,3},{3,0},{4,5},{5,6},{6,7},{7,4},{8,9},{9,10},{10,1... | collective-permute-start | bytes 6684680 | tf_op jit(solution)/shard_map/ppermute | solution.py:21
  70.9 51.4 %collective-permute-start.5 = (f32[128,128,34]{1,0,2:T(8,128)}, f32[128,128,34]{1,0,2:T(8,128)}, u32[]{:S(2)}, u32[]{:S(2)}) collective-permute-start(f32[128,128,34]{1,0,2:T(8,128)} %copy.59), channel_id=1, source_target_pairs={{1,0},{2,1},{3,2},{0,3},{5,4},{6,5},{7,6},{4,7},{9,8},{10,9},{11,1... | collective-permute-start | bytes 6684680 | tf_op jit(solution)/shard_map/ppermute | solution.py:22
  73.6 12.3 %all-to-all-start = ((s32[16,3,4]{2,1,0:T(4,128)}), s32[16,3,4]{2,1,0:T(4,128)S(1)}, u32[]{:S(2)}, u32[]{:S(2)}) async-start(s32[16,3,4]{2,1,0:T(4,128)} %broadcast_in_dim.17), calls=%async_computation | async-start | bytes 65536 | tf_op jit(solution)/shard_map/all_to_all | solution.py:29
  421.1 109.2 %all-to-all-start.1 = ((f32[16,1,110592]{2,1,0:T(1,128)}), f32[16,1,110592]{2,1,0:T(1,128)}, u32[]{:S(2)}, u32[]{:S(2)}) async-start(f32[16,1,110592]{2,1,0:T(1,128)} %reshape.517), calls=%async_computation.1 | async-start | bytes 14155776 | tf_op jit(solution)/shard_map/all_to_all | solution.py:108
where the time goes:
time: 558 us; the launch traced here: 548 us
  local copies, waits for them, and re-layouts  217 us (39%)
  waiting for transfers between devices  166 us (30%)
  matrix products  114 us (20%)
  other arithmetic  27.3 us (5%)
  starting transfers between devices  22.7 us (4%)
    gather x80, local copies, waits for them, and re-layouts  132 us
    all_to_all x1, waiting for transfers between devices, body(): lax.all_to_all(fields.reshape(groups, CAP, G * G * G), 'gx', split_axis=0...  103 us
    ppermute x3, waiting for transfers between devices, padded(): before = lax.ppermute(last, axis, up)  52.9 us
    dot_general x1, matrix products, refine(): step_y = jnp.einsum('by,ayz->abz', matrix, step_x, precision=highest)  45.9 us
    dot_general x1, matrix products, refine(): step_x = jnp.einsum('ax,xyz->ayz', matrix, window, precision=highest)  42.6 us
    dot_general x1, matrix products, refine(): step_z = jnp.einsum('cz,abz->abc', matrix, step_y, precision=highest)  25.6 us
    concatenate x3, other arithmetic, padded(): array = jnp.concatenate([before, array, after], axis=dim)  25.2 us
    reshape x1, local copies, waits for them, and re-layouts, body(): fields.reshape(groups, CAP, G * G * G)  22.5 us
  transfers between devices with their start and end apart: 8, of which 6 were waited for; matrix products, arithmetic and copies ran while one was open for 4% of the time, Pallas kernels for 0%

commit v1 on v0

v1 whole, which is shorter than its diff:
```python
import functools

import jax
import jax.numpy as jnp
import numpy as np
from jax import lax
from jax.experimental import pallas as pl
from jax.experimental.pallas import tpu as pltpu
from jax.sharding import PartitionSpec as P

MESH = pl.DeviceIdType.MESH
G = 48
BOX = 68
HALO = 34
BX = 60
BY = 60
BZ = 128
NX = 960
NY = 120
NZ = 512
GX = 16
SLOTS = 4
EXT = 128
YL = 128
FLAT = 864
SX = 72
LEFT = 12
OWN = 19
PACKS = LEFT + OWN + LEFT
F32 = jnp.float32
BF16 = jnp.bfloat16


def interp_matrix():
    a = np.arange(G)[:, None]
    x = np.arange(BOX)[None, :]
    total = np.ones((G, BOX))
    for k in range(1, G // 2):
        total = total + 2.0 * np.cos(2.0 * np.pi * k * (a / G - x / BOX))
    return (total / BOX).astype(np.float32)


def tables():
    m = interp_matrix()
    ytab = np.zeros((248, 128), np.float32)
    for j in range(248):
        if j % NY < BOX:
            ytab[j, :G] = m[:, j % NY]
    ztab = np.zeros((512, 128), np.float32)
    for j in range(512):
        if j % 256 < BOX:
            ztab[j, :G] = m[:, j % 256]
    mx = np.zeros((G, SX), np.float32)
    mx[:, :BOX] = m
    return ytab, ztab, mx


def split(v):
    hi = v.astype(BF16)
    return hi, (v - hi.astype(F32)).astype(BF16)


def dot(a, b):
    return jnp.dot(a, b, preferred_element_type=F32)


def kernel(
    pot, root, ytab, ztab, mxt, out,
    roots, roots_s, xr, zsend, zrecv, ehi, elo, w_ref, my_ref, s_ref, send, recv,
    root_send, root_recv, local_sem, own_sem, x_send, x_recv, xd_send, xd_recv,
    z_send, z_recv, zd_send, zd_recv, f_send, f_recv,
):
    me = lax.axis_index("gx")
    core = lax.axis_index("gy")
    plane = lax.axis_index("gz")
    my_y, my_x = me // 4, me % 4

    def line(g):
        return {"gx": g, "gy": core, "gz": plane}

    def shifted(k):
        return ((my_y + k // 4) % 4) * 4 + (my_x + k % 4) % 4

    nxt, prv = (me + 1) % GX, (me + GX - 1) % GX
    partner = {"gx": me, "gy": 1 - core, "gz": plane}
    z_up = {"gx": me, "gy": core, "gz": (plane + 1) % 4}
    z_down = {"gx": me, "gy": core, "gz": (plane + 3) % 4}

    barrier = pltpu.get_barrier_semaphore()
    for d in (partner, z_up, z_down):
        pl.semaphore_signal(barrier, inc=1, device_id=d, device_id_type=MESH)

    @pl.loop(1, GX)
    def _(k):
        pl.semaphore_signal(barrier, inc=1, device_id=line(shifted(k)), device_id_type=MESH)

    pl.semaphore_wait(barrier, GX + 2)

    mine = pl.ds(pl.multiple_of(core * 64, 64), BY)
    mine64 = pl.ds(pl.multiple_of(core * 64, 64), 64)

    def remote(src, dst, ssem, rsem, to):
        return pltpu.make_async_remote_copy(
            src_ref=src, dst_ref=dst, send_sem=ssem, recv_sem=rsem, device_id=to, device_id_type=MESH
        )

    x_parts = ((26, 0, 18, nxt), (0, 94, 16, prv), (44, 18, 16, nxt), (16, 110, 18, prv))
    x_copies = [
        remote(pot.at[pl.ds(s, n)], xr.at[pl.ds(e, n), mine], x_send.at[i], x_recv.at[i], line(to))
        for i, (s, e, n, to) in enumerate(x_parts)
    ]
    def root_copy(k):
        return remote(root, roots.at[k], root_send.at[k], root_recv.at[k], line(shifted(k)))

    @pl.loop(1, GX)
    def _(k):
        root_copy(k).start()

    for c in x_copies:
        c.start()
    local = pltpu.make_async_copy(pot, xr.at[pl.ds(HALO, BX), mine], local_sem.at[0])
    local.start()
    own_d2d = remote(pot, xr.at[pl.ds(HALO, BX), mine], own_sem.at[0], own_sem.at[1], partner)
    own_d2d.start()
    roots[0] = root[...]

    local.wait()
    own_d2d.wait_recv()

    @pl.loop(0, EXT)
    def _(x):
        xr[x, 60:64, :] = jnp.zeros((4, 128), F32)
        xr[x, 124:128, :] = jnp.zeros((4, 128), F32)

    lane = lax.broadcasted_iota(jnp.int32, (64, 128), 1)

    def pack(first, count, slab):
        @pl.loop(0, count)
        def _(p):
            x = slab + 3 * p
            up = jnp.zeros((64, 128), F32)
            down = jnp.zeros((64, 128), F32)
            for j in range(3):
                v = xr[x + j, mine64, :]
                low = 94 - 34 * j
                up = jnp.where((lane >= low) & (lane < low + 34), pltpu.roll(v, (128 - 34 * j) % 128, 1), up)
                down = jnp.where((lane >= 34 * j) & (lane < 34 * j + 34), pltpu.roll(v, 34 * j, 1), down)
            zsend[0, first + p] = up
            zsend[1, first + p] = down

    def z_copies(i, first, count):
        rows = pl.ds(first, count)
        return [
            remote(zsend.at[d, rows], zrecv.at[d, rows, mine64], z_send.at[i, d], z_recv.at[i, d], to)
            for d, to in enumerate((z_up, z_down))
        ]

    def z_relays(i, first, count):
        rows = pl.ds(first, count)
        return [
            remote(zrecv.at[d, rows, mine64], zrecv.at[d, rows, mine64], zd_send.at[i, d], zd_recv.at[i, d], partner)
            for d in range(2)
        ]

    def x_relay(i):
        _, e, n, _ = x_parts[i]
        return remote(xr.at[pl.ds(e, n), mine], xr.at[pl.ds(e, n), mine], xd_send.at[i], xd_recv.at[i], partner)

    lane_y = lax.broadcasted_iota(jnp.int32, (YL, 128), 1)

    def convert(first, count, slab):
        @pl.loop(0, count)
        def _(p):
            below = zrecv[0, first + p]
            above = zrecv[1, first + p]
            for j in range(3):
                x = slab + 3 * p + j
                v = xr[x]
                h, l = split(v)
                ehi[x, :, 0:128] = h
                elo[x, :, 0:128] = l
                edge = jnp.where(
                    lane_y < 34,
                    pltpu.roll(above, (128 - 34 * j) % 128, 1),
                    jnp.where(lane_y >= 94, pltpu.roll(below, 34 * j, 1), 0.0),
                )
                h, l = split(edge)
                ehi[x, :, 128:256] = h
                elo[x, :, 128:256] = l

    z_parts = ((0, OWN, 36), (OWN, 6, 0), (OWN + 6, 6, 92), (OWN + 12, 6, 18), (OWN + 18, 6, 110))
    z_all = [z_copies(i, f, n) for i, (f, n, _) in enumerate(z_parts)]
    relays = [z_relays(i, f, n) for i, (f, n, _) in enumerate(z_parts)]
    x_relays = [x_relay(i) for i in range(4)]

    def z_arrived(i):
        for d in range(2):
            z_all[i][d].wait_recv()
            relays[i][d].start()

    pack(*z_parts[0])
    for c in z_all[0]:
        c.start()
    for i in range(4):
        x_copies[i].wait_recv()
        x_relays[i].start()
        pack(*z_parts[i + 1])
        for c in z_all[i + 1]:
            c.start()
        if i == 2:
            z_arrived(0)
    @pl.loop(1, GX)
    def _(k):
        root_copy(k).wait_recv()

    pltpu.sync_copy(roots, roots_s)
    s_ref[...] = jnp.zeros(s_ref.shape, F32)
    for i in range(4):
        x_relays[i].wait_recv()
    for i in range(5):
        if i:
            z_arrived(i)
        if i >= 1:
            for d in range(2):
                relays[i - 1][d].wait_recv()
            convert(*z_parts[i - 1])
    for d in range(2):
        relays[4][d].wait_recv()
    convert(*z_parts[4])

    mx = mxt[...]
    roll_lane = lax.broadcasted_iota(jnp.int32, (SX, 128), 1)

    def f_copy(k):
        return remote(send.at[k], recv.at[k], f_send.at[k], f_recv.at[k], line(shifted(k)))

    def field(k, dest):
        back = ((4 - k // 4) % 4) * 4 + (4 - k % 4) % 4
        rx, ry, rz = jnp.int32(0), jnp.int32(0), jnp.int32(0)
        for s in range(SLOTS):
            fx = roots_s[back, 0, s]
            mine_too = (fx + HALO) % NX // BX == me
            rx = jnp.where(mine_too, fx, rx)
            ry = jnp.where(mine_too, roots_s[back, 1, s], ry)
            rz = jnp.where(mine_too, roots_s[back, 2, s], rz)
        sx = jnp.minimum((rx + HALO - me * BX + NX) % NX, BX - 1)
        sy = ry
        sz = (rz - plane * BZ + NZ) % 256
        my_t = jnp.concatenate([ytab[pl.ds(NY - sy, 64), :], ytab[pl.ds(NY + BY - sy, 64), :]], axis=0)
        my = my_t.T[0:G, :]
        my_hi, my_lo = split(my)
        my_ref[...] = jnp.concatenate([my_hi, my_lo], axis=0)
        z_hi, z_lo = split(ztab[pl.ds(256 - sz, 256), :])
        w_ref[:, 0:128] = z_hi
        w_ref[:, 128:256] = z_lo

        @pl.loop(0, BOX // 4)
        def _(g):
            both = my_ref[...]
            parts = []
            for j in range(4):
                x = sx + 4 * g + j
                t = dot(both, ehi[x])
                parts.append(t[:G] + t[G:] + dot(both[:G], elo[x]))
            hi, lo = split(jnp.concatenate(parts, axis=0))
            q = dot(hi, w_ref[...])
            t = q[:, :128] + q[:, 128:] + dot(lo, w_ref[:, 0:128])
            for j in range(4):
                s_ref[pl.ds(4 * g + j, G, stride=SX), :] = t[G * j : G * j + G]

        @pl.loop(0, 6)
        def _(g):
            tiles = [jnp.zeros((SX, 128), F32) for _ in range(3)]
            for b in range(8):
                off = 48 * b % 128
                at = 48 * b // 128
                v = s_ref[pl.ds(pl.multiple_of((8 * g + b) * SX, 8), SX), :]
                if off:
                    v = pltpu.roll(v, off, 1)
                if off + 48 > 128:
                    tiles[at] = tiles[at] + jnp.where(roll_lane >= off, v, 0.0)
                    tiles[at + 1] = tiles[at + 1] + jnp.where(roll_lane < off, v, 0.0)
                else:
                    tiles[at] = tiles[at] + v
            hi, lo = split(jnp.concatenate(tiles, axis=1))
            o = dot(mx, hi)
            o = o[:G] + o[G:] + dot(mx[:G], lo)
            for t in range(3):
                dest[pl.ds(3 * g + t, G, stride=18), :] = o[:, 128 * t : 128 * t + 128]

    @pl.loop(1, GX)
    def _(k):
        field(k, send.at[k])
        f_copy(k).start()

    field(0, recv.at[0])

    @pl.loop(1, GX)
    def _(k):
        f_copy(k).wait_recv()

    for s in range(SLOTS):
        anchor = (roots_s[0, 0, s] + HALO) % NX // BX
        k = ((my_y - anchor // 4 + 4) % 4) * 4 + (my_x - anchor % 4 + 4) % 4
        out[pl.ds(s, FLAT, stride=4), :] = recv[k]

    @pl.loop(1, GX)
    def _(k):
        f_copy(k).wait_send()
        root_copy(k).wait_send()

    own_d2d.wait_send()
    for i in range(4):
        x_copies[i].wait_send()
        x_relays[i].wait_send()
    for i in range(5):
        for d in range(2):
            z_all[i][d].wait_send()
            relays[i][d].wait_send()


def body(potential, frag_root):
    ytab, ztab, mx = tables()
    mx = jnp.asarray(mx)
    mx_hi, mx_lo = split(mx)
    mxt = jnp.concatenate([mx_hi, mx_lo], axis=0)
    root = jnp.pad(frag_root, ((0, 5), (0, 124)))
    vmem = pl.BlockSpec(memory_space=pltpu.VMEM)
    dma = pltpu.SemaphoreType.DMA
    out = pl.pallas_call(
        kernel,
        out_shape=jax.ShapeDtypeStruct((FLAT * SLOTS, 128), F32),
        in_specs=[pl.BlockSpec(memory_space=pl.ANY), vmem, vmem, vmem, vmem],
        out_specs=vmem,
        scratch_shapes=[
            pltpu.VMEM((GX, 8, 128), jnp.int32),
            pltpu.SMEM((GX, 8, 128), jnp.int32),
            pltpu.VMEM((EXT, YL, 128), F32),
            pltpu.VMEM((2, PACKS, 64, 128), F32),
            pltpu.VMEM((2, PACKS, YL, 128), F32),
            pltpu.VMEM((EXT, YL, 256), BF16),
            pltpu.VMEM((EXT, YL, 256), BF16),
            pltpu.VMEM((256, 256), BF16),
            pltpu.VMEM((2 * G, YL), BF16),
            pltpu.VMEM((G * SX, 128), F32),
            pltpu.VMEM((GX, FLAT, 128), F32),
            pltpu.VMEM((GX, FLAT, 128), F32),
            dma((GX,)), dma((GX,)), dma((1,)), dma((2,)),
            dma((4,)), dma((4,)), dma((4,)), dma((4,)),
            dma((5, 2)), dma((5, 2)), dma((5, 2)), dma((5, 2)),
            dma((GX,)), dma((GX,)),
        ],
        compiler_params=pltpu.CompilerParams(
            collective_id=0, has_side_effects=True, vmem_limit_bytes=66 * 1000 * 1000
        ),
    )(potential, root, jnp.asarray(ytab), jnp.asarray(ztab), mxt)
    return out.reshape(FLAT, SLOTS, 128).transpose(1, 0, 2).reshape(SLOTS, FLAT * 128)


def solution(mesh):
    return jax.shard_map(
        body,
        mesh=mesh,
        in_specs=(P("gx", "gy", "gz"), P(None, ("gx", "gy", "gz"))),
        out_specs=P(("gx", "gy", "gz"), None),
        check_vma=False,
    )
```

time: 558 us -> 203 us (0.36); the launches traced: 548 us -> 202 us
  local copies, waits for them, and re-layouts: 217 us -> 4.07 us
  Pallas kernels: 0 us -> 198 us
  waiting for transfers between devices: 166 us -> 0 us
  matrix products: 114 us -> 0 us
  other arithmetic: 27.3 us -> 0 us
  starting transfers between devices: 22.7 us -> 0 us
    pallas_call x0 -> x1, Pallas kernels: none -> 198 us  [body(): pl.pallas_call(kernel, out_shape=jax.ShapeDtypeStruct((FLAT * SLOTS, 128)...]
    gather x81 -> x0, local copies, waits for them, and re-layouts: 137 us -> none
    dot_general x3 -> x0, matrix products: 114 us -> none  [the longest x1 45.9 us: refine(): step_y = jnp.einsum('by,ayz->abz', matrix, step_x, precision=highest)]
    all_to_all x2 -> x0, waiting for transfers between devices: 110 us -> none  [the longest x1 103 us: body(): lax.all_to_all(fields.reshape(groups, CAP, G * G * G), 'gx', split_axis=0...]
    ppermute x6 -> x0, waiting for transfers between devices: 56.1 us -> none  [the longest x3 52.9 us: padded(): before = lax.ppermute(last, axis, up)]
    slice x5 -> x0, local copies, waits for them, and re-layouts: 25.7 us -> none  [the longest x4 17.6 us: padded(): last = lax.slice_in_dim(array, length - width, length, axis=dim)]
    concatenate x4 -> x0, other arithmetic: 25.3 us -> none  [the longest x3 25.2 us: padded(): array = jnp.concatenate([before, array, after], axis=dim)]
    reshape x1 -> x0, local copies, waits for them, and re-layouts: 22.5 us -> none  [body(): fields.reshape(groups, CAP, G * G * G)]
  transfers between devices with their start and end apart: 8 -> 0, of which waited for: 6 -> 0; matrix products, arithmetic and copies ran while one was open for 4% -> 0% of each run, Pallas kernels for 0% -> 0%
where the time goes in v1:
time: 203 us; the launch traced here: 202 us
  Pallas kernels  198 us (98%)
  local copies, waits for them, and re-layouts  4.07 us (2%)
    pallas_call x1, Pallas kernels, body(): pl.pallas_call(kernel, out_shape=jax.ShapeDtypeStruct((FLAT * SLOTS, 128)...  198 us

profile of v1, /device:TPU:1, one launch (start us, length us, event | category | flops | bytes accessed | tf_op | source)
XLA Modules:
  0.0 202.4 jit_solution(14091368630475958248)
XLA Ops:
  0.0 1.3 pad.4.root
  1.3 198.4 %shard_map.55 = f32[3456,128]{1,0:T(8,128)} custom-call(f32[60,60,128]{2,1,0:T(8,128)} %pot.1, s32[8,128]{1,0:T(8,128)} %pad.4.root, f32[248,128]{1,0:T(8,128)} %constant.9.clone.ytab, f32[512,128]{1,0:T(8,128)} %constant.10.clone.ztab, bf16[96,72]{1,0:T(8,128)(2,1)} %constant.19.mxt), custom_call_target="tpu_custom_call" | custom-call | tf_op jit(solution)/shard_map/pallas_call | solution.py:330
  199.6 2.8 %copy.8 = f32[4,110592]{1,0:T(4,128)} copy(f32[4,110592]{1,0:T(4,128)} %bitcast.5) | data formatting | bytes 3538944

commit v2 on v1

--- a/solution.py
+++ b/solution.py
@@ -24,6 +24,10 @@
 YL = 128
 FLAT = 864
 SX = 72
+ORDER = (6, 14, 9, 11, 10, 2, 8, 5, 15, 7, 13, 1, 3, 4, 12, 0)
+RELAYED = ((6, 5, 1), (14, 15, 3), (9, 5, 4), (11, 15, 12))
+FORWARD = (4, 5, 6, 7)
+GROUP = 17
 LEFT = 12
 OWN = 19
 PACKS = LEFT + OWN + LEFT
@@ -66,9 +70,9 @@
 
 def kernel(
     pot, root, ytab, ztab, mxt, out,
-    roots, roots_s, xr, zsend, zrecv, ehi, elo, w_ref, my_ref, s_ref, send, recv,
+    roots, roots_s, xr, zsend, zrecv, e_ref, w_ref, my_ref, t1h, t1l, s_ref, fields, relay,
     root_send, root_recv, local_sem, own_sem, x_send, x_recv, xd_send, xd_recv,
-    z_send, z_recv, zd_send, zd_recv, f_send, f_recv,
+    z_send, z_recv, zd_send, zd_recv, f_send, f_recv, r_send, r_recv,
 ):
     me = lax.axis_index("gx")
     core = lax.axis_index("gy")
@@ -177,16 +181,16 @@
                 x = slab + 3 * p + j
                 v = xr[x]
                 h, l = split(v)
-                ehi[x, :, 0:128] = h
-                elo[x, :, 0:128] = l
+                e_ref[x, 0:128, 0:128] = h
+                e_ref[x, 128:256, 0:128] = l
                 edge = jnp.where(
                     lane_y < 34,
                     pltpu.roll(above, (128 - 34 * j) % 128, 1),
                     jnp.where(lane_y >= 94, pltpu.roll(below, 34 * j, 1), 0.0),
                 )
                 h, l = split(edge)
-                ehi[x, :, 128:256] = h
-                elo[x, :, 128:256] = l
+                e_ref[x, 0:128, 128:256] = h
+                e_ref[x, 128:256, 128:256] = l
 
     z_parts = ((0, OWN, 36), (OWN, 6, 0), (OWN + 6, 6, 92), (OWN + 12, 6, 18), (OWN + 18, 6, 110))
     z_all = [z_copies(i, f, n) for i, (f, n, _) in enumerate(z_parts)]
@@ -230,11 +234,31 @@
 
     mx = mxt[...]
     roll_lane = lax.broadcasted_iota(jnp.int32, (SX, 128), 1)
-
-    def f_copy(k):
-        return remote(send.at[k], recv.at[k], f_send.at[k], f_recv.at[k], line(shifted(k)))
-
-    def field(k, dest):
+    relay_legs = {k: leg for k, leg, _ in RELAYED}
+
+    def f_copy(i):
+        k = ORDER[i]
+        if k in relay_legs:
+            j = [r[0] for r in RELAYED].index(k)
+            return remote(fields.at[i], relay.at[j], f_send.at[i], r_recv.at[j], line(shifted(relay_legs[k])))
+        return remote(fields.at[i], fields.at[GX + i], f_send.at[i], f_recv.at[i], line(shifted(k)))
+
+    def forward(j):
+        k, _, leg = RELAYED[j]
+        i = ORDER.index(k)
+        return remote(relay.at[j], fields.at[GX + i], r_send.at[j], f_recv.at[i], line(shifted(leg)))
+
+    def arrival(i):
+        return remote(fields.at[i], fields.at[GX + i], f_send.at[i], f_recv.at[i], line(shifted(1)))
+
+    def choose(i, values):
+        total = jnp.int32(0)
+        for c, v in enumerate(values):
+            total = jnp.where(i == c, v, total)
+        return total
+
+    def field(i):
+        k = choose(i, ORDER)
         back = ((4 - k // 4) % 4) * 4 + (4 - k % 4) % 4
         rx, ry, rz = jnp.int32(0), jnp.int32(0), jnp.int32(0)
         for s in range(SLOTS):
@@ -247,34 +271,39 @@
         sy = ry
         sz = (rz - plane * BZ + NZ) % 256
         my_t = jnp.concatenate([ytab[pl.ds(NY - sy, 64), :], ytab[pl.ds(NY + BY - sy, 64), :]], axis=0)
-        my = my_t.T[0:G, :]
-        my_hi, my_lo = split(my)
-        my_ref[...] = jnp.concatenate([my_hi, my_lo], axis=0)
+        my_hi, my_lo = split(my_t.T[0:G, :])
+        my_ref[0:G, 0:128] = my_hi
+        my_ref[0:G, 128:256] = my_hi
+        my_ref[G : 2 * G, 0:128] = my_lo
+        my_ref[G : 2 * G, 128:256] = my_lo
         z_hi, z_lo = split(ztab[pl.ds(256 - sz, 256), :])
         w_ref[:, 0:128] = z_hi
         w_ref[:, 128:256] = z_lo
 
-        @pl.loop(0, BOX // 4)
+        @pl.loop(0, BOX // GROUP)
         def _(g):
             both = my_ref[...]
-            parts = []
-            for j in range(4):
-                x = sx + 4 * g + j
-                t = dot(both, ehi[x])
-                parts.append(t[:G] + t[G:] + dot(both[:G], elo[x]))
-            hi, lo = split(jnp.concatenate(parts, axis=0))
-            q = dot(hi, w_ref[...])
-            t = q[:, :128] + q[:, 128:] + dot(lo, w_ref[:, 0:128])
-            for j in range(4):
-                s_ref[pl.ds(4 * g + j, G, stride=SX), :] = t[G * j : G * j + G]
-
-        @pl.loop(0, 6)
+            for j in range(GROUP):
+                t = dot(both, e_ref[sx + GROUP * g + j])
+                hi, lo = split(t[:G] + t[G:])
+                rows = pl.ds(pl.multiple_of((GROUP * g + j) * G, G), G)
+                t1h[rows, :] = hi
+                t1l[rows, :] = lo
+
+        @pl.loop(0, BOX // GROUP)
         def _(g):
+            rows = pl.ds(pl.multiple_of(GROUP * g * G, G), GROUP * G)
+            q = dot(t1h[rows, :], w_ref[...])
+            t = q[:, :128] + q[:, 128:] + dot(t1l[rows, :], w_ref[:, 0:128])
+            for j in range(GROUP):
+                s_ref[pl.ds(GROUP * g + j, G, stride=SX), :] = t[G * j : G * j + G]
+
+        for g in range(6):
             tiles = [jnp.zeros((SX, 128), F32) for _ in range(3)]
             for b in range(8):
                 off = 48 * b % 128
                 at = 48 * b // 128
-                v = s_ref[pl.ds(pl.multiple_of((8 * g + b) * SX, 8), SX), :]
+                v = s_ref[pl.ds((8 * g + b) * SX, SX), :]
                 if off:
                     v = pltpu.roll(v, off, 1)
                 if off + 48 > 128:
@@ -282,31 +311,42 @@
                     tiles[at + 1] = tiles[at + 1] + jnp.where(roll_lane < off, v, 0.0)
                 else:
                     tiles[at] = tiles[at] + v
-            hi, lo = split(jnp.concatenate(tiles, axis=1))
-            o = dot(mx, hi)
-            o = o[:G] + o[G:] + dot(mx[:G], lo)
+            r = jnp.concatenate([jnp.concatenate(tiles, axis=1), jnp.zeros((8, 384), F32)], axis=0)
+            hi, lo = split(r)
+            o = dot(mx, jnp.concatenate([hi, lo], axis=0))
+            o = o[:G] + o[G:]
             for t in range(3):
-                dest[pl.ds(3 * g + t, G, stride=18), :] = o[:, 128 * t : 128 * t + 128]
-
-    @pl.loop(1, GX)
-    def _(k):
-        field(k, send.at[k])
-        f_copy(k).start()
-
-    field(0, recv.at[0])
-
-    @pl.loop(1, GX)
-    def _(k):
-        f_copy(k).wait_recv()
+                fields[i, pl.ds(3 * g + t, G, stride=18), :] = o[:, 128 * t : 128 * t + 128]
+
+    @pl.loop(0, GX)
+    def _(i):
+        field(i)
+        for c in range(GX - 1):
+
+            @pl.when(i == c)
+            def _():
+                f_copy(c).start()
+                for j, at in enumerate(FORWARD):
+                    if at == c:
+                        f_copy(ORDER.index(RELAYED[j][0])).wait_recv()
+                        forward(j).start()
+
+    for i in range(GX - 1):
+        arrival(i).wait_recv()
 
     for s in range(SLOTS):
         anchor = (roots_s[0, 0, s] + HALO) % NX // BX
         k = ((my_y - anchor // 4 + 4) % 4) * 4 + (my_x - anchor % 4 + 4) % 4
-        out[pl.ds(s, FLAT, stride=4), :] = recv[k]
+        at = choose(k, [GX + ORDER.index(c) if c else ORDER.index(0) for c in range(GX)])
+        out[pl.ds(s, FLAT, stride=4), :] = fields[at]
+
+    for i in range(GX - 1):
+        f_copy(i).wait_send()
+    for j in range(len(RELAYED)):
+        forward(j).wait_send()
 
     @pl.loop(1, GX)
     def _(k):
-        f_copy(k).wait_send()
         root_copy(k).wait_send()
 
     own_d2d.wait_send()
@@ -323,7 +363,10 @@
     ytab, ztab, mx = tables()
     mx = jnp.asarray(mx)
     mx_hi, mx_lo = split(mx)
-    mxt = jnp.concatenate([mx_hi, mx_lo], axis=0)
+    zero = jnp.zeros((G, 8), BF16)
+    mxt = jnp.concatenate(
+        [jnp.concatenate([m, zero, m, zero], axis=1) for m in (mx_hi, mx_lo)], axis=0
+    )
     root = jnp.pad(frag_root, ((0, 5), (0, 124)))
     vmem = pl.BlockSpec(memory_space=pltpu.VMEM)
     dma = pltpu.SemaphoreType.DMA
@@ -338,17 +381,18 @@
             pltpu.VMEM((EXT, YL, 128), F32),
             pltpu.VMEM((2, PACKS, 64, 128), F32),
             pltpu.VMEM((2, PACKS, YL, 128), F32),
-            pltpu.VMEM((EXT, YL, 256), BF16),
-            pltpu.VMEM((EXT, YL, 256), BF16),
+            pltpu.VMEM((EXT, 2 * YL, 256), BF16),
             pltpu.VMEM((256, 256), BF16),
-            pltpu.VMEM((2 * G, YL), BF16),
+            pltpu.VMEM((2 * G, 2 * YL), BF16),
+            pltpu.VMEM((BOX * G, 256), BF16),
+            pltpu.VMEM((BOX * G, 256), BF16),
             pltpu.VMEM((G * SX, 128), F32),
-            pltpu.VMEM((GX, FLAT, 128), F32),
-            pltpu.VMEM((GX, FLAT, 128), F32),
+            pltpu.VMEM((2 * GX, FLAT, 128), F32),
+            pltpu.VMEM((len(RELAYED), FLAT, 128), F32),
             dma((GX,)), dma((GX,)), dma((1,)), dma((2,)),
             dma((4,)), dma((4,)), dma((4,)), dma((4,)),
             dma((5, 2)), dma((5, 2)), dma((5, 2)), dma((5, 2)),
-            dma((GX,)), dma((GX,)),
+            dma((GX,)), dma((GX,)), dma((4,)), dma((4,)),
         ],
         compiler_params=pltpu.CompilerParams(
             collective_id=0, has_side_effects=True, vmem_limit_bytes=66 * 1000 * 1000

time: 203 us -> 156 us (0.77)
  Pallas kernels: 198 us -> 152 us
    pallas_call x1, Pallas kernels: 198 us -> 152 us  [body(): pl.pallas_call(kernel, out_shape=jax.ShapeDtypeStruct((FLAT * SLOTS, 128)...]
where the time goes in v2:
time: 156 us
  Pallas kernels  152 us (97%)
  local copies, waits for them, and re-layouts  4.07 us (3%)
    pallas_call x1, Pallas kernels, body(): pl.pallas_call(kernel, out_shape=jax.ShapeDtypeStruct((FLAT * SLOTS, 128)...  152 us

profile of v2, /device:TPU:1, one launch (start us, length us, event | category | flops | bytes accessed | tf_op | source)
XLA Modules:
  0.0 156.0 jit_solution(18332882150593239610)
XLA Ops:
  0.0 1.3 pad.4.root
  1.3 151.9 %shard_map.55 = f32[3456,128]{1,0:T(8,128)} custom-call(f32[60,60,128]{2,1,0:T(8,128)} %pot.1, s32[8,128]{1,0:T(8,128)} %pad.4.root, f32[248,128]{1,0:T(8,128)} %constant.11.clone.ytab, f32[512,128]{1,0:T(8,128)} %constant.12.clone.ztab, bf16[96,160]{1,0:T(8,128)(2,1)} %constant.23.mxt), custom_call_target="tpu_custom_call" | custom-call | tf_op jit(solution)/shard_map/pallas_call | solution.py:373
  153.2 2.8 %copy.8 = f32[4,110592]{1,0:T(4,128)} copy(f32[4,110592]{1,0:T(4,128)} %bitcast.5) | data formatting | bytes 3538944

commit v3 on v2

--- a/solution.py
+++ b/solution.py
@@ -71,7 +71,7 @@
 def kernel(
     pot, root, ytab, ztab, mxt, out,
     roots, roots_s, xr, zsend, zrecv, e_ref, w_ref, my_ref, t1h, t1l, s_ref, fields, relay,
-    root_send, root_recv, local_sem, own_sem, x_send, x_recv, xd_send, xd_recv,
+    ready, root_send, root_recv, local_sem, own_sem, x_send, x_recv, xd_send, xd_recv,
     z_send, z_recv, zd_send, zd_recv, f_send, f_recv, r_send, r_recv,
 ):
     me = lax.axis_index("gx")
@@ -91,14 +91,12 @@
     z_down = {"gx": me, "gy": core, "gz": (plane + 3) % 4}
 
     barrier = pltpu.get_barrier_semaphore()
-    for d in (partner, z_up, z_down):
+    first = [partner, z_up, z_down, line(nxt), line(prv)] + [line(shifted(k)) for k in (1, 2, 3, 4, 8, 12)]
+    for d in first:
         pl.semaphore_signal(barrier, inc=1, device_id=d, device_id_type=MESH)
-
-    @pl.loop(1, GX)
-    def _(k):
-        pl.semaphore_signal(barrier, inc=1, device_id=line(shifted(k)), device_id_type=MESH)
-
-    pl.semaphore_wait(barrier, GX + 2)
+    pl.semaphore_wait(barrier, len(first))
+    for k in (4, 8, 12):
+        pl.semaphore_signal(ready, inc=1, device_id=line(shifted(k)), device_id_type=MESH)
 
     mine = pl.ds(pl.multiple_of(core * 64, 64), BY)
     mine64 = pl.ds(pl.multiple_of(core * 64, 64), 64)
@@ -108,17 +106,15 @@
             src_ref=src, dst_ref=dst, send_sem=ssem, recv_sem=rsem, device_id=to, device_id_type=MESH
         )
 
-    x_parts = ((26, 0, 18, nxt), (0, 94, 16, prv), (44, 18, 16, nxt), (16, 110, 18, prv))
+    x_parts = (
+        (26, 0, 18, nxt), (0, 94, 16, prv), (44, 18, 9, nxt), (16, 110, 9, prv), (53, 27, 7, nxt), (25, 119, 9, prv)
+    )
     x_copies = [
         remote(pot.at[pl.ds(s, n)], xr.at[pl.ds(e, n), mine], x_send.at[i], x_recv.at[i], line(to))
         for i, (s, e, n, to) in enumerate(x_parts)
     ]
     def root_copy(k):
         return remote(root, roots.at[k], root_send.at[k], root_recv.at[k], line(shifted(k)))
-
-    @pl.loop(1, GX)
-    def _(k):
-        root_copy(k).start()
 
     for c in x_copies:
         c.start()
@@ -127,14 +123,8 @@
     own_d2d = remote(pot, xr.at[pl.ds(HALO, BX), mine], own_sem.at[0], own_sem.at[1], partner)
     own_d2d.start()
     roots[0] = root[...]
-
+    s_ref[...] = jnp.zeros(s_ref.shape, F32)
     local.wait()
-    own_d2d.wait_recv()
-
-    @pl.loop(0, EXT)
-    def _(x):
-        xr[x, 60:64, :] = jnp.zeros((4, 128), F32)
-        xr[x, 124:128, :] = jnp.zeros((4, 128), F32)
 
     lane = lax.broadcasted_iota(jnp.int32, (64, 128), 1)
 
@@ -155,14 +145,14 @@
     def z_copies(i, first, count):
         rows = pl.ds(first, count)
         return [
-            remote(zsend.at[d, rows], zrecv.at[d, rows, mine64], z_send.at[i, d], z_recv.at[i, d], to)
+            remote(zsend.at[d, rows, 0:BY], zrecv.at[d, rows, mine], z_send.at[i, d], z_recv.at[i, d], to)
             for d, to in enumerate((z_up, z_down))
         ]
 
     def z_relays(i, first, count):
         rows = pl.ds(first, count)
         return [
-            remote(zrecv.at[d, rows, mine64], zrecv.at[d, rows, mine64], zd_send.at[i, d], zd_recv.at[i, d], partner)
+            remote(zrecv.at[d, rows, mine], zrecv.at[d, rows, mine], zd_send.at[i, d], zd_recv.at[i, d], partner)
             for d in range(2)
         ]
 
@@ -171,6 +161,7 @@
         return remote(xr.at[pl.ds(e, n), mine], xr.at[pl.ds(e, n), mine], xd_send.at[i], xd_recv.at[i], partner)
 
     lane_y = lax.broadcasted_iota(jnp.int32, (YL, 128), 1)
+    real = lax.broadcasted_iota(jnp.int32, (YL, 128), 0) % 64 < BY
 
     def convert(first, count, slab):
         @pl.loop(0, count)
@@ -179,58 +170,79 @@
             above = zrecv[1, first + p]
             for j in range(3):
                 x = slab + 3 * p + j
-                v = xr[x]
+                v = jnp.where(real, xr[x], 0.0)
                 h, l = split(v)
                 e_ref[x, 0:128, 0:128] = h
                 e_ref[x, 128:256, 0:128] = l
                 edge = jnp.where(
-                    lane_y < 34,
+                    real & (lane_y < 34),
                     pltpu.roll(above, (128 - 34 * j) % 128, 1),
-                    jnp.where(lane_y >= 94, pltpu.roll(below, 34 * j, 1), 0.0),
+                    jnp.where(real & (lane_y >= 94), pltpu.roll(below, 34 * j, 1), 0.0),
                 )
                 h, l = split(edge)
                 e_ref[x, 0:128, 128:256] = h
                 e_ref[x, 128:256, 128:256] = l
 
-    z_parts = ((0, OWN, 36), (OWN, 6, 0), (OWN + 6, 6, 92), (OWN + 12, 6, 18), (OWN + 18, 6, 110))
+    z_parts = ((0, OWN, 36), (19, 6, 0), (25, 6, 92), (31, 3, 18), (34, 3, 110), (37, 3, 27), (40, 3, 119))
     z_all = [z_copies(i, f, n) for i, (f, n, _) in enumerate(z_parts)]
     relays = [z_relays(i, f, n) for i, (f, n, _) in enumerate(z_parts)]
-    x_relays = [x_relay(i) for i in range(4)]
-
-    def z_arrived(i):
-        for d in range(2):
-            z_all[i][d].wait_recv()
-            relays[i][d].start()
-
-    pack(*z_parts[0])
-    for c in z_all[0]:
-        c.start()
-    for i in range(4):
+    x_relays = [x_relay(i) for i in range(6)]
+
+    def x_arrived(i):
         x_copies[i].wait_recv()
         x_relays[i].start()
         pack(*z_parts[i + 1])
         for c in z_all[i + 1]:
             c.start()
-        if i == 2:
-            z_arrived(0)
+
+    def z_arrived(i):
+        for d in range(2):
+            z_all[i][d].wait_recv()
+            relays[i][d].start()
+
+    def complete(i):
+        if i:
+            x_relays[i - 1].wait_recv()
+        for d in range(2):
+            relays[i][d].wait_recv()
+        convert(*z_parts[i])
+
+    pack(*z_parts[0])
+    for c in z_all[0]:
+        c.start()
+    pl.semaphore_wait(ready, 3)
+
+    @pl.loop(1, GX)
+    def _(k):
+        root_copy(k).start()
+
+    x_arrived(0)
+    x_arrived(1)
+    z_arrived(0)
+
     @pl.loop(1, GX)
     def _(k):
         root_copy(k).wait_recv()
 
     pltpu.sync_copy(roots, roots_s)
-    s_ref[...] = jnp.zeros(s_ref.shape, F32)
-    for i in range(4):
-        x_relays[i].wait_recv()
-    for i in range(5):
-        if i:
-            z_arrived(i)
-        if i >= 1:
-            for d in range(2):
-                relays[i - 1][d].wait_recv()
-            convert(*z_parts[i - 1])
-    for d in range(2):
-        relays[4][d].wait_recv()
-    convert(*z_parts[4])
+    own_d2d.wait_recv()
+    complete(0)
+    x_arrived(2)
+    x_arrived(3)
+    z_arrived(1)
+    z_arrived(2)
+    x_arrived(4)
+    x_arrived(5)
+    complete(1)
+    complete(2)
+    z_arrived(3)
+    z_arrived(4)
+    complete(3)
+    complete(4)
+    z_arrived(5)
+    z_arrived(6)
+    complete(5)
+    complete(6)
 
     mx = mxt[...]
     roll_lane = lax.broadcasted_iota(jnp.int32, (SX, 128), 1)
@@ -280,19 +292,15 @@
         w_ref[:, 0:128] = z_hi
         w_ref[:, 128:256] = z_lo
 
-        @pl.loop(0, BOX // GROUP)
-        def _(g):
-            both = my_ref[...]
+        both = my_ref[...]
+        for g in range(BOX // GROUP):
             for j in range(GROUP):
                 t = dot(both, e_ref[sx + GROUP * g + j])
                 hi, lo = split(t[:G] + t[G:])
-                rows = pl.ds(pl.multiple_of((GROUP * g + j) * G, G), G)
+                rows = pl.ds((GROUP * g + j) * G, G)
                 t1h[rows, :] = hi
                 t1l[rows, :] = lo
-
-        @pl.loop(0, BOX // GROUP)
-        def _(g):
-            rows = pl.ds(pl.multiple_of(GROUP * g * G, G), GROUP * G)
+            rows = pl.ds(GROUP * g * G, GROUP * G)
             q = dot(t1h[rows, :], w_ref[...])
             t = q[:, :128] + q[:, 128:] + dot(t1l[rows, :], w_ref[:, 0:128])
             for j in range(GROUP):
@@ -350,10 +358,10 @@
         root_copy(k).wait_send()
 
     own_d2d.wait_send()
-    for i in range(4):
+    for i in range(6):
         x_copies[i].wait_send()
         x_relays[i].wait_send()
-    for i in range(5):
+    for i in range(7):
         for d in range(2):
             z_all[i][d].wait_send()
             relays[i][d].wait_send()
@@ -367,7 +375,6 @@
     mxt = jnp.concatenate(
         [jnp.concatenate([m, zero, m, zero], axis=1) for m in (mx_hi, mx_lo)], axis=0
     )
-    root = jnp.pad(frag_root, ((0, 5), (0, 124)))
     vmem = pl.BlockSpec(memory_space=pltpu.VMEM)
     dma = pltpu.SemaphoreType.DMA
     out = pl.pallas_call(
@@ -376,8 +383,8 @@
         in_specs=[pl.BlockSpec(memory_space=pl.ANY), vmem, vmem, vmem, vmem],
         out_specs=vmem,
         scratch_shapes=[
-            pltpu.VMEM((GX, 8, 128), jnp.int32),
-            pltpu.SMEM((GX, 8, 128), jnp.int32),
+            pltpu.VMEM((GX, 3, SLOTS), jnp.int32),
+            pltpu.SMEM((GX, 3, SLOTS), jnp.int32),
             pltpu.VMEM((EXT, YL, 128), F32),
             pltpu.VMEM((2, PACKS, 64, 128), F32),
             pltpu.VMEM((2, PACKS, YL, 128), F32),
@@ -389,15 +396,15 @@
             pltpu.VMEM((G * SX, 128), F32),
             pltpu.VMEM((2 * GX, FLAT, 128), F32),
             pltpu.VMEM((len(RELAYED), FLAT, 128), F32),
-            dma((GX,)), dma((GX,)), dma((1,)), dma((2,)),
-            dma((4,)), dma((4,)), dma((4,)), dma((4,)),
-            dma((5, 2)), dma((5, 2)), dma((5, 2)), dma((5, 2)),
+            pltpu.SemaphoreType.REGULAR, dma((GX,)), dma((GX,)), dma((1,)), dma((2,)),
+            dma((6,)), dma((6,)), dma((6,)), dma((6,)),
+            dma((7, 2)), dma((7, 2)), dma((7, 2)), dma((7, 2)),
             dma((GX,)), dma((GX,)), dma((4,)), dma((4,)),
         ],
         compiler_params=pltpu.CompilerParams(
             collective_id=0, has_side_effects=True, vmem_limit_bytes=66 * 1000 * 1000
         ),
-    )(potential, root, jnp.asarray(ytab), jnp.asarray(ztab), mxt)
+    )(potential, frag_root, jnp.asarray(ytab), jnp.asarray(ztab), mxt)
     return out.reshape(FLAT, SLOTS, 128).transpose(1, 0, 2).reshape(SLOTS, FLAT * 128)
 
 

time: 156 us -> 145 us (0.929)
  the two profiles are of different devices: /device:TPU:1 before, /device:TPU:12 now
where the time goes in v3:
time: 145 us
  Pallas kernels  142 us (98%)
  local copies, waits for them, and re-layouts  2.8 us (2%)
    pallas_call x1, Pallas kernels, body(): pl.pallas_call(kernel, out_shape=jax.ShapeDtypeStruct((FLAT * SLOTS, 128)...  142 us

profile of v3, /device:TPU:12, one launch (start us, length us, event | category | flops | bytes accessed | tf_op | source)
XLA Modules:
  0.0 145.3 jit_solution(10452580629466127647)
XLA Ops:
  0.0 142.5 %shard_map.55 = f32[3456,128]{1,0:T(8,128)} custom-call(f32[60,60,128]{2,1,0:T(8,128)} %pot.1, s32[3,4]{1,0:T(4,128)} %root.1, f32[248,128]{1,0:T(8,128)} %constant.9.clone.ytab, f32[512,128]{1,0:T(8,128)} %constant.10.clone.ztab, bf16[96,160]{1,0:T(8,128)(2,1)} %constant.19.mxt), custom_call_target="tpu_custom_call" | custom-call | tf_op jit(solution)/shard_map/pallas_call | solution.py:380
  142.5 2.8 %copy.8 = f32[4,110592]{1,0:T(4,128)} copy(f32[4,110592]{1,0:T(4,128)} %bitcast.5) | data formatting | bytes 3538944

commit v4 on v3

--- a/solution.py
+++ b/solution.py
@@ -28,9 +28,8 @@
 RELAYED = ((6, 5, 1), (14, 15, 3), (9, 5, 4), (11, 15, 12))
 FORWARD = (4, 5, 6, 7)
 GROUP = 17
-LEFT = 12
-OWN = 19
-PACKS = LEFT + OWN + LEFT
+UNITS = 19
+OFFSETS = (0, 34, 68, 102, 8, 42, 76)
 F32 = jnp.float32
 BF16 = jnp.bfloat16
 
@@ -107,7 +106,7 @@
         )
 
     x_parts = (
-        (26, 0, 18, nxt), (0, 94, 16, prv), (44, 18, 9, nxt), (16, 110, 9, prv), (53, 27, 7, nxt), (25, 119, 9, prv)
+        (26, 0, 14, nxt), (0, 94, 13, prv), (40, 14, 14, nxt), (13, 107, 14, prv), (54, 28, 6, nxt), (27, 121, 7, prv)
     )
     x_copies = [
         remote(pot.at[pl.ds(s, n)], xr.at[pl.ds(e, n), mine], x_send.at[i], x_recv.at[i], line(to))
@@ -123,34 +122,37 @@
     own_d2d = remote(pot, xr.at[pl.ds(HALO, BX), mine], own_sem.at[0], own_sem.at[1], partner)
     own_d2d.start()
     roots[0] = root[...]
-    s_ref[...] = jnp.zeros(s_ref.shape, F32)
     local.wait()
 
     lane = lax.broadcasted_iota(jnp.int32, (64, 128), 1)
 
     def pack(first, count, slab):
         @pl.loop(0, count)
-        def _(p):
-            x = slab + 3 * p
-            up = jnp.zeros((64, 128), F32)
-            down = jnp.zeros((64, 128), F32)
-            for j in range(3):
-                v = xr[x + j, mine64, :]
-                low = 94 - 34 * j
-                up = jnp.where((lane >= low) & (lane < low + 34), pltpu.roll(v, (128 - 34 * j) % 128, 1), up)
-                down = jnp.where((lane >= 34 * j) & (lane < 34 * j + 34), pltpu.roll(v, 34 * j, 1), down)
-            zsend[0, first + p] = up
-            zsend[1, first + p] = down
+        def _(u):
+            tiles = [[jnp.zeros((64, 128), F32) for _ in range(2)] for _ in range(2)]
+            for j, off in enumerate(OFFSETS):
+                v = xr[slab + 7 * u + j, mine64, :]
+                for d, at in enumerate((off - 94, off)):
+                    w = pltpu.roll(v, at % 128, 1) if at % 128 else v
+                    if j == 3:
+                        tiles[d][0] = jnp.where(lane >= off, w, tiles[d][0])
+                        tiles[d][1] = jnp.where(lane < off + 34 - 128, w, tiles[d][1])
+                    else:
+                        inside = (lane >= off) & (lane < off + 34)
+                        tiles[d][j // 4] = jnp.where(inside, w, tiles[d][j // 4])
+            for d in range(2):
+                for t in range(2):
+                    zsend[d, 2 * (first + u) + t] = tiles[d][t]
 
     def z_copies(i, first, count):
-        rows = pl.ds(first, count)
+        rows = pl.ds(2 * first, 2 * count)
         return [
             remote(zsend.at[d, rows, 0:BY], zrecv.at[d, rows, mine], z_send.at[i, d], z_recv.at[i, d], to)
             for d, to in enumerate((z_up, z_down))
         ]
 
     def z_relays(i, first, count):
-        rows = pl.ds(first, count)
+        rows = pl.ds(2 * first, 2 * count)
         return [
             remote(zrecv.at[d, rows, mine], zrecv.at[d, rows, mine], zd_send.at[i, d], zd_recv.at[i, d], partner)
             for d in range(2)
@@ -161,32 +163,38 @@
         return remote(xr.at[pl.ds(e, n), mine], xr.at[pl.ds(e, n), mine], xd_send.at[i], xd_recv.at[i], partner)
 
     lane_y = lax.broadcasted_iota(jnp.int32, (YL, 128), 1)
-    real = lax.broadcasted_iota(jnp.int32, (YL, 128), 0) % 64 < BY
-
-    def convert(first, count, slab):
-        @pl.loop(0, count)
+    def convert_own(slab, count):
+        @pl.loop(0, count // 2)
         def _(p):
-            below = zrecv[0, first + p]
-            above = zrecv[1, first + p]
-            for j in range(3):
-                x = slab + 3 * p + j
-                v = jnp.where(real, xr[x], 0.0)
-                h, l = split(v)
+            for j in range(2):
+                x = slab + 2 * p + j
+                h, l = split(xr[x])
                 e_ref[x, 0:128, 0:128] = h
                 e_ref[x, 128:256, 0:128] = l
-                edge = jnp.where(
-                    real & (lane_y < 34),
-                    pltpu.roll(above, (128 - 34 * j) % 128, 1),
-                    jnp.where(real & (lane_y >= 94), pltpu.roll(below, 34 * j, 1), 0.0),
-                )
-                h, l = split(edge)
+
+    def convert_edges(first, count, slab):
+        @pl.loop(0, count)
+        def _(u):
+            below = [zrecv[0, 2 * (first + u) + t] for t in range(2)]
+            above = [zrecv[1, 2 * (first + u) + t] for t in range(2)]
+            for j, off in enumerate(OFFSETS):
+                x = slab + 7 * u + j
+                parts = []
+                for tiles, at in ((above, -off), (below, 94 - off)):
+                    v = jnp.where(lane_y >= off, tiles[0], tiles[1]) if j == 3 else tiles[j // 4]
+                    parts.append(pltpu.roll(v, at % 128, 1) if at % 128 else v)
+                h, l = split(jnp.where(lane_y < 34, parts[0], jnp.where(lane_y >= 94, parts[1], 0.0)))
                 e_ref[x, 0:128, 128:256] = h
                 e_ref[x, 128:256, 128:256] = l
 
-    z_parts = ((0, OWN, 36), (19, 6, 0), (25, 6, 92), (31, 3, 18), (34, 3, 110), (37, 3, 27), (40, 3, 119))
+    z_parts = ((0, 9, 35), (9, 2, 0), (11, 2, 93), (13, 2, 14), (15, 2, 107), (17, 1, 28), (18, 1, 121))
     z_all = [z_copies(i, f, n) for i, (f, n, _) in enumerate(z_parts)]
     relays = [z_relays(i, f, n) for i, (f, n, _) in enumerate(z_parts)]
     x_relays = [x_relay(i) for i in range(6)]
+
+    def own_units(work):
+        work(0, 8, 35)
+        work(8, 1, 87)
 
     def x_arrived(i):
         x_copies[i].wait_recv()
@@ -195,54 +203,82 @@
         for c in z_all[i + 1]:
             c.start()
 
+    def x_complete(i):
+        x_relays[i].wait_recv()
+        _, e, n, _ = x_parts[i]
+        convert_own(e - e % 2 if e > 90 and n == 7 else e - n % 2, n + n % 2)
+
     def z_arrived(i):
         for d in range(2):
             z_all[i][d].wait_recv()
             relays[i][d].start()
 
-    def complete(i):
-        if i:
-            x_relays[i - 1].wait_recv()
+    def z_complete(i):
         for d in range(2):
             relays[i][d].wait_recv()
-        convert(*z_parts[i])
-
-    pack(*z_parts[0])
+        if i:
+            convert_edges(*z_parts[i])
+        else:
+            own_units(convert_edges)
+
+    own_units(pack)
     for c in z_all[0]:
         c.start()
+
+    @pl.loop(0, EXT)
+    def _(x):
+        xr[x, 60:64, :] = jnp.zeros((4, 128), F32)
+        xr[x, 124:128, :] = jnp.zeros((4, 128), F32)
+
+    @pl.loop(0, 2 * UNITS)
+    def _(t):
+        for d in range(2):
+            zrecv[d, t, 60:64, :] = jnp.zeros((4, 128), F32)
+            zrecv[d, t, 124:128, :] = jnp.zeros((4, 128), F32)
+
+    s_ref[...] = jnp.zeros(s_ref.shape, F32)
     pl.semaphore_wait(ready, 3)
 
     @pl.loop(1, GX)
     def _(k):
         root_copy(k).start()
 
+    own_d2d.wait_recv()
+    convert_own(HALO, BX)
     x_arrived(0)
     x_arrived(1)
     z_arrived(0)
-
-    @pl.loop(1, GX)
-    def _(k):
-        root_copy(k).wait_recv()
-
-    pltpu.sync_copy(roots, roots_s)
-    own_d2d.wait_recv()
-    complete(0)
+    x_complete(0)
+    x_complete(1)
+    z_complete(0)
     x_arrived(2)
     x_arrived(3)
     z_arrived(1)
     z_arrived(2)
+    x_complete(2)
+    x_complete(3)
+    z_complete(1)
+    z_complete(2)
     x_arrived(4)
     x_arrived(5)
-    complete(1)
-    complete(2)
     z_arrived(3)
     z_arrived(4)
-    complete(3)
-    complete(4)
+    x_complete(4)
+    x_complete(5)
+
+    @pl.loop(1, GX)
+    def _(k):
+        root_copy(k).wait_recv()
+
+    roots_copy = pltpu.make_async_copy(roots, roots_s, local_sem.at[1])
+    roots_copy.start()
+    z_complete(3)
+    z_complete(4)
     z_arrived(5)
     z_arrived(6)
-    complete(5)
-    complete(6)
+    z_complete(5)
+    z_complete(6)
+    roots_copy.wait()
 
     mx = mxt[...]
     roll_lane = lax.broadcasted_iota(jnp.int32, (SX, 128), 1)
@@ -386,8 +422,8 @@
             pltpu.VMEM((GX, 3, SLOTS), jnp.int32),
             pltpu.SMEM((GX, 3, SLOTS), jnp.int32),
             pltpu.VMEM((EXT, YL, 128), F32),
-            pltpu.VMEM((2, PACKS, 64, 128), F32),
-            pltpu.VMEM((2, PACKS, YL, 128), F32),
+            pltpu.VMEM((2, 2 * UNITS, 64, 128), F32),
+            pltpu.VMEM((2, 2 * UNITS, YL, 128), F32),
             pltpu.VMEM((EXT, 2 * YL, 256), BF16),
             pltpu.VMEM((256, 256), BF16),
             pltpu.VMEM((2 * G, 2 * YL), BF16),
@@ -396,7 +432,7 @@
             pltpu.VMEM((G * SX, 128), F32),
             pltpu.VMEM((2 * GX, FLAT, 128), F32),
             pltpu.VMEM((len(RELAYED), FLAT, 128), F32),
-            pltpu.SemaphoreType.REGULAR, dma((GX,)), dma((GX,)), dma((1,)), dma((2,)),
+            pltpu.SemaphoreType.REGULAR, dma((GX,)), dma((GX,)), dma((2,)), dma((2,)),
             dma((6,)), dma((6,)), dma((6,)), dma((6,)),
             dma((7, 2)), dma((7, 2)), dma((7, 2)), dma((7, 2)),
             dma((GX,)), dma((GX,)), dma((4,)), dma((4,)),

time: 145 us -> 138 us (0.952)
  the two profiles are of different devices: /device:TPU:12 before, /device:TPU:1 now
where the time goes in v4:
time: 138 us; the launch traced here: 136 us
  Pallas kernels  133 us (96%)
  local copies, waits for them, and re-layouts  2.8 us (2%)
    pallas_call x1, Pallas kernels, body(): pl.pallas_call(kernel, out_shape=jax.ShapeDtypeStruct((FLAT * SLOTS, 128)...  133 us
    unnamed x1, local copies, waits for them, and re-layouts  2.8 us

profile of v4, /device:TPU:1, one launch (start us, length us, event | category | flops | bytes accessed | tf_op | source)
XLA Modules:
  0.0 136.0 jit_solution(5648495681068464366)
XLA Ops:
  0.0 133.2 %shard_map.55 = f32[3456,128]{1,0:T(8,128)} custom-call(f32[60,60,128]{2,1,0:T(8,128)} %pot.1, s32[3,4]{1,0:T(4,128)} %root.1, f32[248,128]{1,0:T(8,128)} %constant.9.clone.ytab, f32[512,128]{1,0:T(8,128)} %constant.10.clone.ztab, bf16[96,160]{1,0:T(8,128)(2,1)} %constant.19.mxt), custom_call_target="tpu_custom_call" | custom-call | tf_op jit(solution)/shard_map/pallas_call | solution.py:416
  133.2 2.8 %copy.8 = f32[4,110592]{1,0:T(4,128)} copy(f32[4,110592]{1,0:T(4,128)} %bitcast.5) | data formatting | bytes 3538944

commit v5 on v4

--- a/solution.py
+++ b/solution.py
@@ -24,9 +24,9 @@
 YL = 128
 FLAT = 864
 SX = 72
-ORDER = (6, 14, 9, 11, 10, 2, 8, 5, 15, 7, 13, 1, 3, 4, 12, 0)
+ORDER = (10, 6, 14, 9, 11, 5, 15, 7, 13, 2, 8, 1, 3, 4, 12, 0)
 RELAYED = ((6, 5, 1), (14, 15, 3), (9, 5, 4), (11, 15, 12))
-FORWARD = (4, 5, 6, 7)
+FORWARD = (7, 8, 9, 10)
 GROUP = 17
 UNITS = 19
 OFFSETS = (0, 34, 68, 102, 8, 42, 76)
@@ -93,12 +93,41 @@
     first = [partner, z_up, z_down, line(nxt), line(prv)] + [line(shifted(k)) for k in (1, 2, 3, 4, 8, 12)]
     for d in first:
         pl.semaphore_signal(barrier, inc=1, device_id=d, device_id_type=MESH)
+    mine = pl.ds(pl.multiple_of(core * 64, 64), BY)
+
+    local = pltpu.make_async_copy(pot, xr.at[pl.ds(HALO, BX), mine], local_sem.at[0])
+    local.start()
+    lane = lax.broadcasted_iota(jnp.int32, (32, 128), 1)
+
+    def pack(first, count, slab):
+        @pl.loop(0, count)
+        def _(u):
+            for part in range(2):
+                here = pl.ds(pl.multiple_of(core * 64 + 32 * part, 32), 32)
+                tiles = [[jnp.zeros((32, 128), F32) for _ in range(2)] for _ in range(2)]
+                for j, off in enumerate(OFFSETS):
+                    v = xr[slab + 7 * u + j, here, :]
+                    for d, at in enumerate((off - 94, off)):
+                        w = pltpu.roll(v, at % 128, 1) if at % 128 else v
+                        if j == 3:
+                            tiles[d][0] = jnp.where(lane >= off, w, tiles[d][0])
+                            tiles[d][1] = jnp.where(lane < off + 34 - 128, w, tiles[d][1])
+                        else:
+                            inside = (lane >= off) & (lane < off + 34)
+                            tiles[d][j // 4] = jnp.where(inside, w, tiles[d][j // 4])
+                for d in range(2):
+                    for t in range(2):
+                        zsend[d, 2 * (first + u) + t, 32 * part : 32 * part + 32] = tiles[d][t]
+
+    def own_units(work):
+        work(0, 8, 35)
+        work(8, 1, 87)
+
+    local.wait()
+    own_units(pack)
     pl.semaphore_wait(barrier, len(first))
     for k in (4, 8, 12):
         pl.semaphore_signal(ready, inc=1, device_id=line(shifted(k)), device_id_type=MESH)
-
-    mine = pl.ds(pl.multiple_of(core * 64, 64), BY)
-    mine64 = pl.ds(pl.multiple_of(core * 64, 64), 64)
 
     def remote(src, dst, ssem, rsem, to):
         return pltpu.make_async_remote_copy(
@@ -117,32 +146,9 @@
 
     for c in x_copies:
         c.start()
-    local = pltpu.make_async_copy(pot, xr.at[pl.ds(HALO, BX), mine], local_sem.at[0])
-    local.start()
     own_d2d = remote(pot, xr.at[pl.ds(HALO, BX), mine], own_sem.at[0], own_sem.at[1], partner)
     own_d2d.start()
     roots[0] = root[...]
-    local.wait()
-
-    lane = lax.broadcasted_iota(jnp.int32, (64, 128), 1)
-
-    def pack(first, count, slab):
-        @pl.loop(0, count)
-        def _(u):
-            tiles = [[jnp.zeros((64, 128), F32) for _ in range(2)] for _ in range(2)]
-            for j, off in enumerate(OFFSETS):
-                v = xr[slab + 7 * u + j, mine64, :]
-                for d, at in enumerate((off - 94, off)):
-                    w = pltpu.roll(v, at % 128, 1) if at % 128 else v
-                    if j == 3:
-                        tiles[d][0] = jnp.where(lane >= off, w, tiles[d][0])
-                        tiles[d][1] = jnp.where(lane < off + 34 - 128, w, tiles[d][1])
-                    else:
-                        inside = (lane >= off) & (lane < off + 34)
-                        tiles[d][j // 4] = jnp.where(inside, w, tiles[d][j // 4])
-            for d in range(2):
-                for t in range(2):
-                    zsend[d, 2 * (first + u) + t] = tiles[d][t]
 
     def z_copies(i, first, count):
         rows = pl.ds(2 * first, 2 * count)
@@ -162,7 +168,6 @@
         _, e, n, _ = x_parts[i]
         return remote(xr.at[pl.ds(e, n), mine], xr.at[pl.ds(e, n), mine], xd_send.at[i], xd_recv.at[i], partner)
 
-    lane_y = lax.broadcasted_iota(jnp.int32, (YL, 128), 1)
     def convert_own(slab, count):
         @pl.loop(0, count // 2)
         def _(p):
@@ -175,26 +180,24 @@
     def convert_edges(first, count, slab):
         @pl.loop(0, count)
         def _(u):
-            below = [zrecv[0, 2 * (first + u) + t] for t in range(2)]
-            above = [zrecv[1, 2 * (first + u) + t] for t in range(2)]
-            for j, off in enumerate(OFFSETS):
-                x = slab + 7 * u + j
-                parts = []
-                for tiles, at in ((above, -off), (below, 94 - off)):
-                    v = jnp.where(lane_y >= off, tiles[0], tiles[1]) if j == 3 else tiles[j // 4]
-                    parts.append(pltpu.roll(v, at % 128, 1) if at % 128 else v)
-                h, l = split(jnp.where(lane_y < 34, parts[0], jnp.where(lane_y >= 94, parts[1], 0.0)))
-                e_ref[x, 0:128, 128:256] = h
-                e_ref[x, 128:256, 128:256] = l
+            for part in range(4):
+                here = pl.ds(32 * part, 32)
+                below = [zrecv[0, 2 * (first + u) + t, here, :] for t in range(2)]
+                above = [zrecv[1, 2 * (first + u) + t, here, :] for t in range(2)]
+                for j, off in enumerate(OFFSETS):
+                    x = slab + 7 * u + j
+                    both = []
+                    for tiles, at in ((above, -off), (below, 94 - off)):
+                        v = jnp.where(lane >= off, tiles[0], tiles[1]) if j == 3 else tiles[j // 4]
+                        both.append(pltpu.roll(v, at % 128, 1) if at % 128 else v)
+                    h, l = split(jnp.where(lane < 34, both[0], jnp.where(lane >= 94, both[1], 0.0)))
+                    e_ref[x, 32 * part : 32 * part + 32, 128:256] = h
+                    e_ref[x, 128 + 32 * part : 160 + 32 * part, 128:256] = l
 
     z_parts = ((0, 9, 35), (9, 2, 0), (11, 2, 93), (13, 2, 14), (15, 2, 107), (17, 1, 28), (18, 1, 121))
     z_all = [z_copies(i, f, n) for i, (f, n, _) in enumerate(z_parts)]
     relays = [z_relays(i, f, n) for i, (f, n, _) in enumerate(z_parts)]
     x_relays = [x_relay(i) for i in range(6)]
-
-    def own_units(work):
-        work(0, 8, 35)
-        work(8, 1, 87)
 
     def x_arrived(i):
         x_copies[i].wait_recv()
@@ -221,7 +224,6 @@
         else:
             own_units(convert_edges)
 
-    own_units(pack)
     for c in z_all[0]:
         c.start()
 

time: 138 us -> 131 us (0.949)
  Pallas kernels: 133 us -> 128 us
    pallas_call x1, Pallas kernels: 133 us -> 128 us  [body(): pl.pallas_call(kernel, out_shape=jax.ShapeDtypeStruct((FLAT * SLOTS, 128)...]
where the time goes in v5:
time: 131 us; the launch traced here: 130 us
  Pallas kernels  128 us (98%)
  local copies, waits for them, and re-layouts  2.8 us (2%)
    pallas_call x1, Pallas kernels, body(): pl.pallas_call(kernel, out_shape=jax.ShapeDtypeStruct((FLAT * SLOTS, 128)...  128 us
    unnamed x1, local copies, waits for them, and re-layouts  2.8 us

profile of v5, /device:TPU:1, one launch (start us, length us, event | category | flops | bytes accessed | tf_op | source)
XLA Modules:
  0.0 130.4 jit_solution(3442664551006988148)
XLA Ops:
  0.0 127.6 %shard_map.55 = f32[3456,128]{1,0:T(8,128)} custom-call(f32[60,60,128]{2,1,0:T(8,128)} %pot.1, s32[3,4]{1,0:T(4,128)} %root.1, f32[248,128]{1,0:T(8,128)} %constant.9.clone.ytab, f32[512,128]{1,0:T(8,128)} %constant.10.clone.ztab, bf16[96,160]{1,0:T(8,128)(2,1)} %constant.19.mxt), custom_call_target="tpu_custom_call" | custom-call | tf_op jit(solution)/shard_map/pallas_call | solution.py:418
  127.6 2.8 %copy.8 = f32[4,110592]{1,0:T(4,128)} copy(f32[4,110592]{1,0:T(4,128)} %bitcast.5) | data formatting | bytes 3538944

commit v6 on v5

--- a/solution.py
+++ b/solution.py
@@ -23,6 +23,8 @@
 EXT = 128
 YL = 128
 FLAT = 864
+PLANE = 18
+SENT = FLAT - PLANE
 SX = 72
 ORDER = (10, 6, 14, 9, 11, 5, 15, 7, 13, 2, 8, 1, 3, 4, 12, 0)
 RELAYED = ((6, 5, 1), (14, 15, 3), (9, 5, 4), (11, 15, 12))
@@ -68,11 +70,15 @@
 
 
 def kernel(
-    pot, root, ytab, ztab, mxt, out,
-    roots, roots_s, xr, zsend, zrecv, e_ref, w_ref, my_ref, t1h, t1l, s_ref, fields, relay,
-    ready, root_send, root_recv, local_sem, own_sem, x_send, x_recv, xd_send, xd_recv,
+    pot, root, ytab_in, ztab_in, mxt_in, out,
+    ytab, ztab, mxt, stage, roots, roots_s, xr, zsend, zrecv, e_ref, w_ref, my_ref, t1h, t1l, s_ref, fields, relay,
+    table_sem, out_sem, ready, root_send, root_recv, local_sem, own_sem, x_send, x_recv, xd_send, xd_recv,
     z_send, z_recv, zd_send, zd_recv, f_send, f_recv, r_send, r_recv,
 ):
+    tables_in = [
+        pltpu.make_async_copy(a, b, table_sem.at[i])
+        for i, (a, b) in enumerate(((ytab_in, ytab), (ztab_in, ztab), (mxt_in, mxt), (root, roots.at[0])))
+    ]
     me = lax.axis_index("gx")
     core = lax.axis_index("gy")
     plane = lax.axis_index("gz")
@@ -123,6 +129,8 @@
         work(0, 8, 35)
         work(8, 1, 87)
 
+    for c in tables_in:
+        c.start()
     local.wait()
     own_units(pack)
     pl.semaphore_wait(barrier, len(first))
@@ -148,7 +156,6 @@
         c.start()
     own_d2d = remote(pot, xr.at[pl.ds(HALO, BX), mine], own_sem.at[0], own_sem.at[1], partner)
     own_d2d.start()
-    roots[0] = root[...]
 
     def z_copies(i, first, count):
         rows = pl.ds(2 * first, 2 * count)
@@ -272,6 +279,8 @@
     def _(k):
         root_copy(k).wait_recv()
 
+    for c in tables_in:
+        c.wait()
     roots_copy = pltpu.make_async_copy(roots, roots_s, local_sem.at[1])
     roots_copy.start()
     z_complete(3)
@@ -284,22 +293,23 @@
 
     mx = mxt[...]
     roll_lane = lax.broadcasted_iota(jnp.int32, (SX, 128), 1)
+    sent = pl.ds(0, SENT)
     relay_legs = {k: leg for k, leg, _ in RELAYED}
 
     def f_copy(i):
         k = ORDER[i]
         if k in relay_legs:
             j = [r[0] for r in RELAYED].index(k)
-            return remote(fields.at[i], relay.at[j], f_send.at[i], r_recv.at[j], line(shifted(relay_legs[k])))
-        return remote(fields.at[i], fields.at[GX + i], f_send.at[i], f_recv.at[i], line(shifted(k)))
+            return remote(fields.at[i, sent], relay.at[j], f_send.at[i], r_recv.at[j], line(shifted(relay_legs[k])))
+        return remote(fields.at[i, sent], fields.at[GX + i, sent], f_send.at[i], f_recv.at[i], line(shifted(k)))
 
     def forward(j):
         k, _, leg = RELAYED[j]
         i = ORDER.index(k)
-        return remote(relay.at[j], fields.at[GX + i], r_send.at[j], f_recv.at[i], line(shifted(leg)))
+        return remote(relay.at[j], fields.at[GX + i, sent], r_send.at[j], f_recv.at[i], line(shifted(leg)))
 
     def arrival(i):
-        return remote(fields.at[i], fields.at[GX + i], f_send.at[i], f_recv.at[i], line(shifted(1)))
+        return remote(fields.at[i, sent], fields.at[GX + i, sent], f_send.at[i], f_recv.at[i], line(shifted(1)))
 
     def choose(i, values):
         total = jnp.int32(0)
@@ -380,11 +390,26 @@
     for i in range(GX - 1):
         arrival(i).wait_recv()
 
+    places = []
     for s in range(SLOTS):
         anchor = (roots_s[0, 0, s] + HALO) % NX // BX
         k = ((my_y - anchor // 4 + 4) % 4) * 4 + (my_x - anchor % 4 + 4) % 4
-        at = choose(k, [GX + ORDER.index(c) if c else ORDER.index(0) for c in range(GX)])
-        out[pl.ds(s, FLAT, stride=4), :] = fields[at]
+        places.append(choose(k, [GX + ORDER.index(c) if c else ORDER.index(0) for c in range(GX)]))
+
+    out_copies = []
+    for c in range(4):
+        n = 216 if c < 3 else 216 - PLANE
+        for s, at in enumerate(places):
+            stage[pl.ds(864 * c + s, n, stride=4), :] = fields[at, 216 * c : 216 * c + n]
+            if c == 3:
+                for r in range(PLANE):
+                    even = fields[at, pl.ds(r, 24, stride=2 * PLANE), :]
+                    odd = fields[at, pl.ds(r + PLANE, 23, stride=2 * PLANE), :]
+                    last = jnp.sum(even, axis=0, keepdims=True) - jnp.sum(odd, axis=0, keepdims=True)
+                    stage[pl.ds(4 * (SENT + r) + s, 1), :] = last
+        rows = pl.ds(864 * c, 864)
+        out_copies.append(pltpu.make_async_copy(stage.at[rows], out.at[rows], out_sem.at[c]))
+        out_copies[c].start()
 
     for i in range(GX - 1):
         f_copy(i).wait_send()
@@ -395,6 +420,8 @@
     def _(k):
         root_copy(k).wait_send()
 
+    for c in out_copies:
+        c.wait()
     own_d2d.wait_send()
     for i in range(6):
         x_copies[i].wait_send()
@@ -413,14 +440,17 @@
     mxt = jnp.concatenate(
         [jnp.concatenate([m, zero, m, zero], axis=1) for m in (mx_hi, mx_lo)], axis=0
     )
-    vmem = pl.BlockSpec(memory_space=pltpu.VMEM)
     dma = pltpu.SemaphoreType.DMA
     out = pl.pallas_call(
         kernel,
         out_shape=jax.ShapeDtypeStruct((FLAT * SLOTS, 128), F32),
-        in_specs=[pl.BlockSpec(memory_space=pl.ANY), vmem, vmem, vmem, vmem],
-        out_specs=vmem,
+        in_specs=[pl.BlockSpec(memory_space=pl.ANY)] * 5,
+        out_specs=pl.BlockSpec(memory_space=pl.ANY),
         scratch_shapes=[
+            pltpu.VMEM((248, 128), F32),
+            pltpu.VMEM((512, 128), F32),
+            pltpu.VMEM(mxt.shape, BF16),
+            pltpu.VMEM((FLAT * SLOTS, 128), F32),
             pltpu.VMEM((GX, 3, SLOTS), jnp.int32),
             pltpu.SMEM((GX, 3, SLOTS), jnp.int32),
             pltpu.VMEM((EXT, YL, 128), F32),
@@ -433,7 +463,8 @@
             pltpu.VMEM((BOX * G, 256), BF16),
             pltpu.VMEM((G * SX, 128), F32),
             pltpu.VMEM((2 * GX, FLAT, 128), F32),
-            pltpu.VMEM((len(RELAYED), FLAT, 128), F32),
+            pltpu.VMEM((len(RELAYED), SENT, 128), F32),
+            dma((4,)), dma((4,)),
             pltpu.SemaphoreType.REGULAR, dma((GX,)), dma((GX,)), dma((2,)), dma((2,)),
             dma((6,)), dma((6,)), dma((6,)), dma((6,)),
             dma((7, 2)), dma((7, 2)), dma((7, 2)), dma((7, 2)),

time: 131 us -> 128 us (0.977)
  Pallas kernels: 128 us -> 125 us
    pallas_call x1, Pallas kernels: 128 us -> 125 us  [body(): pl.pallas_call(kernel, out_shape=jax.ShapeDtypeStruct((FLAT * SLOTS, 128)...]
where the time goes in v6:
time: 128 us
  Pallas kernels  125 us (98%)
  local copies, waits for them, and re-layouts  2.8 us (2%)
    pallas_call x1, Pallas kernels, body(): pl.pallas_call(kernel, out_shape=jax.ShapeDtypeStruct((FLAT * SLOTS, 128)...  125 us
    unnamed x1, local copies, waits for them, and re-layouts  2.8 us

profile of v6, /device:TPU:1, one launch (start us, length us, event | category | flops | bytes accessed | tf_op | source)
XLA Modules:
  0.0 127.8 jit_solution(14026478003248731868)
XLA Ops:
  0.0 125.0 %shard_map.55 = f32[3456,128]{1,0:T(8,128)} custom-call(f32[60,60,128]{2,1,0:T(8,128)} %pot.1, s32[3,4]{1,0:T(4,128)} %root.1, f32[248,128]{1,0:T(8,128)} %constant.9.clone.ytab_in, f32[512,128]{1,0:T(8,128)} %constant.10.clone.ztab_in, bf16[96,160]{1,0:T(8,128)(2,1)} %constant.19.mxt_in), custom_call_target="tpu_custom_call" | custom-call | tf_op jit(solution)/shard_map/pallas_call | solution.py:444
  125.0 2.8 %copy.8 = f32[4,110592]{1,0:T(4,128)} copy(f32[4,110592]{1,0:T(4,128)} %bitcast.5) | data formatting | bytes 3538944

commit v7 on v6

--- a/solution.py
+++ b/solution.py
@@ -72,7 +72,7 @@
 def kernel(
     pot, root, ytab_in, ztab_in, mxt_in, out,
     ytab, ztab, mxt, stage, roots, roots_s, xr, zsend, zrecv, e_ref, w_ref, my_ref, t1h, t1l, s_ref, fields, relay,
-    table_sem, out_sem, ready, root_send, root_recv, local_sem, own_sem, x_send, x_recv, xd_send, xd_recv,
+    table_sem, out_sem, ready, ready_z, root_send, root_recv, local_sem, own_sem, x_send, x_recv, xd_send, xd_recv,
     z_send, z_recv, zd_send, zd_recv, f_send, f_recv, r_send, r_recv,
 ):
     tables_in = [
@@ -126,14 +126,18 @@
                         zsend[d, 2 * (first + u) + t, 32 * part : 32 * part + 32] = tiles[d][t]
 
     def own_units(work):
-        work(0, 8, 35)
+        work(0, 8, 34)
         work(8, 1, 87)
 
     for c in tables_in:
         c.start()
     local.wait()
     own_units(pack)
+    pack(17, 1, 87)
+    pack(18, 1, 61)
     pl.semaphore_wait(barrier, len(first))
+    for d in (z_up, z_down):
+        pl.semaphore_signal(ready_z, inc=1, device_id=d, device_id_type=MESH)
     for k in (4, 8, 12):
         pl.semaphore_signal(ready, inc=1, device_id=line(shifted(k)), device_id_type=MESH)
 
@@ -143,7 +147,8 @@
         )
 
     x_parts = (
-        (26, 0, 14, nxt), (0, 94, 13, prv), (40, 14, 14, nxt), (13, 107, 14, prv), (54, 28, 6, nxt), (27, 121, 7, prv)
+        (26, 0, 14, nxt), (0, 94, 13, prv), (40, 14, 7, nxt), (13, 107, 7, prv),
+        (47, 21, 7, nxt), (20, 114, 7, prv), (54, 28, 6, nxt), (27, 121, 7, prv),
     )
     x_copies = [
         remote(pot.at[pl.ds(s, n)], xr.at[pl.ds(e, n), mine], x_send.at[i], x_recv.at[i], line(to))
@@ -152,16 +157,19 @@
     def root_copy(k):
         return remote(root, roots.at[k], root_send.at[k], root_recv.at[k], line(shifted(k)))
 
-    for c in x_copies:
+    for c in x_copies[:6]:
         c.start()
     own_d2d = remote(pot, xr.at[pl.ds(HALO, BX), mine], own_sem.at[0], own_sem.at[1], partner)
     own_d2d.start()
 
-    def z_copies(i, first, count):
+    def z_copies(i, first, count, line_to):
         rows = pl.ds(2 * first, 2 * count)
         return [
-            remote(zsend.at[d, rows, 0:BY], zrecv.at[d, rows, mine], z_send.at[i, d], z_recv.at[i, d], to)
-            for d, to in enumerate((z_up, z_down))
+            remote(
+                zsend.at[d, rows, 0:BY], zrecv.at[d, rows, mine], z_send.at[i, d], z_recv.at[i, d],
+                {"gx": line_to, "gy": core, "gz": (plane + step) % 4},
+            )
+            for d, step in enumerate((1, 3))
         ]
 
     def z_relays(i, first, count):
@@ -201,22 +209,28 @@
                     e_ref[x, 32 * part : 32 * part + 32, 128:256] = h
                     e_ref[x, 128 + 32 * part : 160 + 32 * part, 128:256] = l
 
-    z_parts = ((0, 9, 35), (9, 2, 0), (11, 2, 93), (13, 2, 14), (15, 2, 107), (17, 1, 28), (18, 1, 121))
-    z_all = [z_copies(i, f, n) for i, (f, n, _) in enumerate(z_parts)]
+    z_parts = (
+        (0, 9, 34), (9, 2, 0), (11, 2, 93), (13, 1, 14), (14, 1, 107), (15, 1, 21), (16, 1, 114),
+        (17, 1, 27), (18, 1, 121),
+    )
+    z_all = [
+        z_copies(i, f, n, me if i < 7 else nxt if i == 7 else prv) for i, (f, n, _) in enumerate(z_parts)
+    ]
     relays = [z_relays(i, f, n) for i, (f, n, _) in enumerate(z_parts)]
-    x_relays = [x_relay(i) for i in range(6)]
+    x_relays = [x_relay(i) for i in range(8)]
 
     def x_arrived(i):
         x_copies[i].wait_recv()
         x_relays[i].start()
-        pack(*z_parts[i + 1])
-        for c in z_all[i + 1]:
-            c.start()
+        if i < 6:
+            pack(*z_parts[i + 1])
+            for c in z_all[i + 1]:
+                c.start()
 
     def x_complete(i):
         x_relays[i].wait_recv()
         _, e, n, _ = x_parts[i]
-        convert_own(e - e % 2 if e > 90 and n == 7 else e - n % 2, n + n % 2)
+        convert_own(e - n % 2, n + n % 2)
 
     def z_arrived(i):
         for d in range(2):
@@ -234,6 +248,10 @@
     for c in z_all[0]:
         c.start()
 
+    pl.semaphore_wait(ready_z, 2)
+    for c in z_all[7] + z_all[8] + x_copies[6:]:
+        c.start()
+
     @pl.loop(0, EXT)
     def _(x):
         xr[x, 60:64, :] = jnp.zeros((4, 128), F32)
@@ -259,22 +277,31 @@
     z_arrived(0)
     x_complete(0)
     x_complete(1)
-    z_complete(0)
     x_arrived(2)
     x_arrived(3)
+    z_complete(0)
     z_arrived(1)
     z_arrived(2)
     x_complete(2)
     x_complete(3)
+    x_arrived(4)
+    x_arrived(5)
     z_complete(1)
     z_complete(2)
-    x_arrived(4)
-    x_arrived(5)
     z_arrived(3)
     z_arrived(4)
     x_complete(4)
     x_complete(5)
-
+    z_complete(3)
+    z_complete(4)
+    z_arrived(7)
+    z_arrived(8)
+    z_arrived(5)
+    z_arrived(6)
+    x_arrived(6)
+    x_arrived(7)
+    z_complete(7)
+    z_complete(8)
     @pl.loop(1, GX)
     def _(k):
         root_copy(k).wait_recv()
@@ -283,12 +310,10 @@
         c.wait()
     roots_copy = pltpu.make_async_copy(roots, roots_s, local_sem.at[1])
     roots_copy.start()
-    z_complete(3)
-    z_complete(4)
-    z_arrived(5)
-    z_arrived(6)
     z_complete(5)
     z_complete(6)
+    x_complete(6)
+    x_complete(7)
     roots_copy.wait()
 
     mx = mxt[...]
@@ -423,10 +448,10 @@
     for c in out_copies:
         c.wait()
     own_d2d.wait_send()
-    for i in range(6):
+    for i in range(8):
         x_copies[i].wait_send()
         x_relays[i].wait_send()
-    for i in range(7):
+    for i in range(9):
         for d in range(2):
             z_all[i][d].wait_send()
             relays[i][d].wait_send()
@@ -465,9 +490,9 @@
             pltpu.VMEM((2 * GX, FLAT, 128), F32),
             pltpu.VMEM((len(RELAYED), SENT, 128), F32),
             dma((4,)), dma((4,)),
-            pltpu.SemaphoreType.REGULAR, dma((GX,)), dma((GX,)), dma((2,)), dma((2,)),
-            dma((6,)), dma((6,)), dma((6,)), dma((6,)),
-            dma((7, 2)), dma((7, 2)), dma((7, 2)), dma((7, 2)),
+            pltpu.SemaphoreType.REGULAR, pltpu.SemaphoreType.REGULAR, dma((GX,)), dma((GX,)), dma((2,)), dma((2,)),
+            dma((8,)), dma((8,)), dma((8,)), dma((8,)),
+            dma((9, 2)), dma((9, 2)), dma((9, 2)), dma((9, 2)),
             dma((GX,)), dma((GX,)), dma((4,)), dma((4,)),
         ],
         compiler_params=pltpu.CompilerParams(

time: 128 us -> 126 us (0.984)
  Pallas kernels: 125 us -> 123 us
    pallas_call x1, Pallas kernels: 125 us -> 123 us  [body(): pl.pallas_call(kernel, out_shape=jax.ShapeDtypeStruct((FLAT * SLOTS, 128)...]
where the time goes in v7:
time: 126 us
  Pallas kernels  123 us (98%)
  local copies, waits for them, and re-layouts  2.8 us (2%)
    pallas_call x1, Pallas kernels, body(): pl.pallas_call(kernel, out_shape=jax.ShapeDtypeStruct((FLAT * SLOTS, 128)...  123 us
    unnamed x1, local copies, waits for them, and re-layouts  2.8 us

profile of v7, /device:TPU:1, one launch (start us, length us, event | category | flops | bytes accessed | tf_op | source)
XLA Modules:
  0.0 126.1 jit_solution(1657351715374305747)
XLA Ops:
  0.0 123.3 %shard_map.55 = f32[3456,128]{1,0:T(8,128)} custom-call(f32[60,60,128]{2,1,0:T(8,128)} %pot.1, s32[3,4]{1,0:T(4,128)} %root.1, f32[248,128]{1,0:T(8,128)} %constant.9.clone.ytab_in, f32[512,128]{1,0:T(8,128)} %constant.10.clone.ztab_in, bf16[96,160]{1,0:T(8,128)(2,1)} %constant.19.mxt_in), custom_call_target="tpu_custom_call" | custom-call | tf_op jit(solution)/shard_map/pallas_call | solution.py:469
  123.3 2.8 %copy.8 = f32[4,110592]{1,0:T(4,128)} copy(f32[4,110592]{1,0:T(4,128)} %bitcast.5) | data formatting | bytes 3538944

commit v8 on v7

--- a/solution.py
+++ b/solution.py
@@ -113,14 +113,16 @@
                 tiles = [[jnp.zeros((32, 128), F32) for _ in range(2)] for _ in range(2)]
                 for j, off in enumerate(OFFSETS):
                     v = xr[slab + 7 * u + j, here, :]
-                    for d, at in enumerate((off - 94, off)):
-                        w = pltpu.roll(v, at % 128, 1) if at % 128 else v
-                        if j == 3:
-                            tiles[d][0] = jnp.where(lane >= off, w, tiles[d][0])
-                            tiles[d][1] = jnp.where(lane < off + 34 - 128, w, tiles[d][1])
-                        else:
-                            inside = (lane >= off) & (lane < off + 34)
-                            tiles[d][j // 4] = jnp.where(inside, w, tiles[d][j // 4])
+                    w = pltpu.roll(v, off, 1) if off else v
+                    if j == 3:
+                        tiles[0][0] = jnp.where((lane >= 68) & (lane < 94), w, tiles[0][0])
+                        tiles[0][1] = jnp.where((lane >= 94) & (lane < 102), w, tiles[0][1])
+                        tiles[1][0] = jnp.where(lane >= 102, w, tiles[1][0])
+                        tiles[1][1] = jnp.where(lane < 8, w, tiles[1][1])
+                    else:
+                        t = j // 4
+                        tiles[0][t] = jnp.where((lane + 34 - off) % 128 < 34, w, tiles[0][t])
+                        tiles[1][t] = jnp.where((lane >= off) & (lane < off + 34), w, tiles[1][t])
                 for d in range(2):
                     for t in range(2):
                         zsend[d, 2 * (first + u) + t, 32 * part : 32 * part + 32] = tiles[d][t]
@@ -201,11 +203,12 @@
                 above = [zrecv[1, 2 * (first + u) + t, here, :] for t in range(2)]
                 for j, off in enumerate(OFFSETS):
                     x = slab + 7 * u + j
-                    both = []
-                    for tiles, at in ((above, -off), (below, 94 - off)):
-                        v = jnp.where(lane >= off, tiles[0], tiles[1]) if j == 3 else tiles[j // 4]
-                        both.append(pltpu.roll(v, at % 128, 1) if at % 128 else v)
-                    h, l = split(jnp.where(lane < 34, both[0], jnp.where(lane >= 94, both[1], 0.0)))
+                    if j == 3:
+                        v = jnp.where(lane < 94, below[0], below[1])
+                        v = jnp.where(lane < 8, above[1], jnp.where(lane >= 102, above[0], v))
+                    else:
+                        v = jnp.where((lane >= off) & (lane < off + 34), above[j // 4], below[j // 4])
+                    h, l = split(pltpu.roll(v, 128 - off, 1) if off else v)
                     e_ref[x, 32 * part : 32 * part + 32, 128:256] = h
                     e_ref[x, 128 + 32 * part : 160 + 32 * part, 128:256] = l
 

time: 126 us -> 126 us (level)
  no operation moved by 1% of the time
where the time goes in v8:
time: 126 us; the launch traced here: 125 us
  Pallas kernels  123 us (98%)
  local copies, waits for them, and re-layouts  2.8 us (2%)
    pallas_call x1, Pallas kernels, body(): pl.pallas_call(kernel, out_shape=jax.ShapeDtypeStruct((FLAT * SLOTS, 128)...  123 us
    unnamed x1, local copies, waits for them, and re-layouts  2.8 us

profile of v8, /device:TPU:1, one launch (start us, length us, event | category | flops | bytes accessed | tf_op | source)
XLA Modules:
  0.0 125.5 jit_solution(11592629938730125863)
XLA Ops:
  0.0 122.7 %shard_map.55 = f32[3456,128]{1,0:T(8,128)} custom-call(f32[60,60,128]{2,1,0:T(8,128)} %pot.1, s32[3,4]{1,0:T(4,128)} %root.1, f32[248,128]{1,0:T(8,128)} %constant.9.clone.ytab_in, f32[512,128]{1,0:T(8,128)} %constant.10.clone.ztab_in, bf16[96,160]{1,0:T(8,128)(2,1)} %constant.19.mxt_in), custom_call_target="tpu_custom_call" | custom-call | tf_op jit(solution)/shard_map/pallas_call | solution.py:472
  122.7 2.8 %copy.8 = f32[4,110592]{1,0:T(4,128)} copy(f32[4,110592]{1,0:T(4,128)} %bitcast.5) | data formatting | bytes 3538944

commit v9 on v8

--- a/solution.py
+++ b/solution.py
@@ -251,6 +251,12 @@
     for c in z_all[0]:
         c.start()
 
+    pl.semaphore_wait(ready, 3)
+
+    @pl.loop(1, GX)
+    def _(k):
+        root_copy(k).start()
+
     pl.semaphore_wait(ready_z, 2)
     for c in z_all[7] + z_all[8] + x_copies[6:]:
         c.start()
@@ -267,12 +273,6 @@
             zrecv[d, t, 124:128, :] = jnp.zeros((4, 128), F32)
 
     s_ref[...] = jnp.zeros(s_ref.shape, F32)
-    pl.semaphore_wait(ready, 3)
-
-    @pl.loop(1, GX)
-    def _(k):
-        root_copy(k).start()
-
     own_d2d.wait_recv()
     convert_own(HALO, BX)
     x_arrived(0)
@@ -301,18 +301,18 @@
     z_arrived(8)
     z_arrived(5)
     z_arrived(6)
+    @pl.loop(1, GX)
+    def _(k):
+        root_copy(k).wait_recv()
+
+    for c in tables_in:
+        c.wait()
+    roots_copy = pltpu.make_async_copy(roots, roots_s, local_sem.at[1])
+    roots_copy.start()
     x_arrived(6)
     x_arrived(7)
     z_complete(7)
     z_complete(8)
-    @pl.loop(1, GX)
-    def _(k):
-        root_copy(k).wait_recv()
-
-    for c in tables_in:
-        c.wait()
-    roots_copy = pltpu.make_async_copy(roots, roots_s, local_sem.at[1])
-    roots_copy.start()
     z_complete(5)
     z_complete(6)
     x_complete(6)

time: 126 us -> 126 us (level)
  no operation moved by 1% of the time
where the time goes in v9:
time: 126 us; the launch traced here: 125 us
  Pallas kernels  123 us (98%)
  local copies, waits for them, and re-layouts  2.8 us (2%)
    pallas_call x1, Pallas kernels, body(): pl.pallas_call(kernel, out_shape=jax.ShapeDtypeStruct((FLAT * SLOTS, 128)...  123 us
    unnamed x1, local copies, waits for them, and re-layouts  2.8 us

profile of v9, /device:TPU:1, one launch (start us, length us, event | category | flops | bytes accessed | tf_op | source)
XLA Modules:
  0.0 125.5 jit_solution(11145260041010927754)
XLA Ops:
  0.0 122.7 %shard_map.55 = f32[3456,128]{1,0:T(8,128)} custom-call(f32[60,60,128]{2,1,0:T(8,128)} %pot.1, s32[3,4]{1,0:T(4,128)} %root.1, f32[248,128]{1,0:T(8,128)} %constant.9.clone.ytab_in, f32[512,128]{1,0:T(8,128)} %constant.10.clone.ztab_in, bf16[96,160]{1,0:T(8,128)(2,1)} %constant.19.mxt_in), custom_call_target="tpu_custom_call" | custom-call | tf_op jit(solution)/shard_map/pallas_call | solution.py:472
  122.7 2.8 %copy.8 = f32[4,110592]{1,0:T(4,128)} copy(f32[4,110592]{1,0:T(4,128)} %bitcast.5) | data formatting | bytes 3538944
